TPU v7x, 32 devices: a whole 2x2x4 slice. The times are simulated.
32 devices in a mesh: patch: 8 (over z, y), hidden: 4 (over x, core).
Axes of the slice: x: 2, y: 2, z: 4, core: 2. Of those that a mesh axis runs over, the one named last changes fastest.
Arguments:
- grid_latent: bfloat16 [24576, 512], P('patch'), may hold values from -6 to 6
- mesh_latent: bfloat16 [40960, 512], P('patch'), may hold values from -6 to 6
- edge_latent: bfloat16 [65536, 512], P('patch'), may hold values from -6 to 6
- senders: int32 [65536], P('patch'), may hold values from 0 to 24575, as said below
- receivers: int32 [65536], P('patch'), may hold values from 0 to 40959
- mesh_slot: int32 [40960], replicated, may hold values from 0 to 40959, as said below
- edge_counts: int32 [8], P('patch'), may hold values from 2730 to 8192, as said below
- w_edge: bfloat16 [512, 512], P(None, 'hidden'), may hold values from -0.25 to 0.25
- w_sender: bfloat16 [512, 512], P(None, 'hidden'), may hold values from -0.25 to 0.25
- w_receiver: bfloat16 [512, 512], P(None, 'hidden'), may hold values from -0.25 to 0.25
- edge_bias: float32 [512], P('hidden'), may hold values from -3 to 3
- w_edge_out: bfloat16 [512, 512], P('hidden'), may hold values from -0.25 to 0.25
- edge_out_bias: float32 [512], P('hidden'), may hold values from -3 to 3
- edge_gain: float32 [512], P('hidden'), may hold values from 0.25 to 1.75
- edge_shift: float32 [512], P('hidden'), may hold values from -2 to 2
- w_mesh_in: bfloat16 [512, 512], P(None, 'hidden'), may hold values from -0.25 to 0.25
- w_message_in: bfloat16 [512, 512], P(None, 'hidden'), may hold values from -0.25 to 0.25
- mesh_bias: float32 [512], P('hidden'), may hold values from -3 to 3
- w_mesh_out: bfloat16 [512, 512], P('hidden'), may hold values from -0.25 to 0.25
- mesh_out_bias: float32 [512], P('hidden'), may hold values from -3 to 3
- mesh_gain: float32 [512], P('hidden'), may hold values from 0.25 to 1.75
- mesh_shift: float32 [512], P('hidden'), may hold values from -2 to 2
Outputs:
- mesh_out: bfloat16 [40960, 512], P('patch', 'hidden')
- edge_out: bfloat16 [65536, 512], P('patch', 'hidden')
Inputs may be any that keep to these rules, and one draw needn't show every extreme that they name: `mesh_slot`: A permutation of the mesh node ids 0 to 40959; owner block p holds mesh rows p * 5120 to (p + 1) * 5120 - 1. `senders`: edge slots of block p (slots p * 8192 to (p + 1) * 8192 - 1) send from grid nodes p * 3072 to (p + 1) * 3072 - 1. Only the first edge_counts[p] slots of block p are live; some block is full.
All inputs are finite; a program needn't handle non-finite values.
Results may differ from a plain program's by a relative error of at most 0.014.
Values may be sent and summed in bfloat16 or wider, within the bound.
A program may use at most 192 MiB of HBM per device.

v0:
```python
import jax
import jax.numpy as jnp
from jax import lax
from jax.sharding import PartitionSpec as P

EPSILON = 1e-05


def as_sent(x):
    return jax.tree.map(lambda a: a.astype(jnp.bfloat16) if a.dtype == jnp.float32 else a, x)


def normalize(values, gain, offset, width, total_fn):
    totals = total_fn((jnp.sum(values, axis=1), jnp.sum(values * values, axis=1)))
    center = totals[0] / width
    spread = jnp.maximum(totals[1] / width - center * center, 0.0)
    centered = values - center[:, None]
    return centered * lax.rsqrt(spread + EPSILON)[:, None] * gain + offset


def edge_totals(values):
    return jax.tree.map(lambda part: part.astype(jnp.float32), lax.psum(as_sent(values), "hidden"))


def mesh_totals(values):
    return lax.psum(values, "hidden")


def shards(
    grid_latent,
    mesh_latent,
    edge_latent,
    senders,
    receivers,
    mesh_slot,
    edge_counts,
    w_edge,
    w_sender,
    w_receiver,
    edge_bias,
    w_edge_out,
    edge_out_bias,
    edge_gain,
    edge_shift,
    w_mesh_in,
    w_message_in,
    mesh_bias,
    w_mesh_out,
    mesh_out_bias,
    mesh_gain,
    mesh_shift,
):
    patch_index = lax.axis_index("patch")
    column_index = lax.axis_index("hidden")
    own_grid = grid_latent.shape[0]
    own_edges = edge_latent.shape[0]
    slice_width = w_edge.shape[1]
    full_width = w_edge.shape[0]
    mesh_total = mesh_slot.shape[0]
    target_rows = jnp.take(mesh_slot, receivers)
    sender_local = senders - patch_index * own_grid
    live = (jnp.arange(own_edges, dtype=jnp.int32) < edge_counts[0]).astype(jnp.float32)
    receiver_part = jnp.dot(mesh_latent, w_receiver, preferred_element_type=jnp.float32).astype(
        jnp.bfloat16
    )
    table = lax.all_gather(receiver_part, "patch", axis=0, tiled=True)
    sender_part = jnp.dot(grid_latent, w_sender, preferred_element_type=jnp.float32)
    edge_pre = jnp.dot(edge_latent, w_edge, preferred_element_type=jnp.float32)
    edge_pre = (
        edge_pre
        + jnp.take(sender_part, sender_local, axis=0)
        + jnp.take(table, target_rows, axis=0).astype(jnp.float32)
        + edge_bias
    )
    edge_hidden = jax.nn.silu(edge_pre).astype(jnp.bfloat16)
    edge_partial = jnp.dot(edge_hidden, w_edge_out, preferred_element_type=jnp.float32)
    edge_summed = (
        lax.psum_scatter(
            edge_partial.astype(jnp.bfloat16), "hidden", scatter_dimension=1, tiled=True
        ).astype(jnp.float32)
        + edge_out_bias
    )
    message = normalize(edge_summed, edge_gain, edge_shift, full_width, edge_totals) * live[:, None]
    own_edge_cols = lax.dynamic_slice_in_dim(
        edge_latent, column_index * slice_width, slice_width, 1
    )
    edge_out = (own_edge_cols.astype(jnp.float32) + message).astype(jnp.bfloat16)
    spread_sums = jax.ops.segment_sum(message, target_rows, num_segments=mesh_total)
    received = lax.psum_scatter(
        spread_sums.astype(jnp.bfloat16), "patch", scatter_dimension=0, tiled=True
    )
    mesh_pre = jnp.dot(mesh_latent, w_mesh_in, preferred_element_type=jnp.float32) + mesh_bias
    gathered = lax.all_gather(received, "hidden", axis=1, tiled=True)
    mesh_pre = mesh_pre + jnp.dot(gathered, w_message_in, preferred_element_type=jnp.float32)
    mesh_hidden = jax.nn.silu(mesh_pre).astype(jnp.bfloat16)
    mesh_partial = jnp.dot(mesh_hidden, w_mesh_out, preferred_element_type=jnp.float32)
    mesh_summed = (
        lax.psum_scatter(
            mesh_partial.astype(jnp.bfloat16), "hidden", scatter_dimension=1, tiled=True
        ).astype(jnp.float32)
        + mesh_out_bias
    )
    mesh_update = normalize(mesh_summed, mesh_gain, mesh_shift, full_width, mesh_totals)
    own_mesh_cols = lax.dynamic_slice_in_dim(
        mesh_latent, column_index * slice_width, slice_width, 1
    )
    mesh_out = (own_mesh_cols.astype(jnp.float32) + mesh_update).astype(jnp.bfloat16)
    return (mesh_out, edge_out)


def solution(mesh):
    return jax.shard_map(
        shards,
        mesh=mesh,
        in_specs=(
            P("patch", None),
            P("patch", None),
            P("patch", None),
            P("patch"),
            P("patch"),
            P(),
            P("patch"),
            P(None, "hidden"),
            P(None, "hidden"),
            P(None, "hidden"),
            P("hidden"),
            P("hidden", None),
            P("hidden"),
            P("hidden"),
            P("hidden"),
            P(None, "hidden"),
            P(None, "hidden"),
            P("hidden"),
            P("hidden", None),
            P("hidden"),
            P("hidden"),
            P("hidden"),
        ),
        out_specs=(P("patch", "hidden"), P("patch", "hidden")),
        check_vma=False,
    )
```

profile of v0, /device:TPU:0, one launch (start us, length us, event | category | flops | bytes accessed | tf_op | source)
XLA Modules:
  0.0 686.1 jit_solution(1188223292079852615)
XLA Ops:
  7.2 0.0 copy-start
  7.2 0.0 copy-start.7
  7.2 0.0 copy-start.2
  7.2 0.0 all-gather.3.cloned.1.call-start
  7.2 5.2 convolution_convert_fusion.2
  12.5 0.0 all-gather.3.cloned.1.call-update
  12.5 0.0 reduce-scatter.10.cloned.1.call-start
  12.5 0.0 copy-done.7
  12.6 0.0 copy-done.2
  12.6 0.0 copy-start.6
  12.6 0.0 copy-start.4
  12.6 80.5 %gather_fusion = s32[8192]{0:T(1024)} fusion(s32[40960]{0:T(1024)S(1)} %copy-done.2, s32[8192]{0:T(1024)S(1)} %fusion.21), kind=kCustom, calls=%fused_computation | custom fusion | bytes 98304 | tf_op jit(solution)/shard_map/jit(_take)/gather | solution.py:60
  93.1 0.0 copy-done.6
  93.1 0.0 copy-done
  93.2 0.0 copy-done.4
  93.2 2.1 fusion.28
  95.3 29.2 %gather_fusion.1 = f32[8192,128]{1,0:T(8,128)} fusion(f32[3072,128]{1,0:T(8,128)} %fusion.28, s32[8192]{0:T(1024)S(1)} %fusion.23), kind=kCustom, calls=%fused_computation.1 | custom fusion | bytes 8421376 | tf_op jit(solution)/shard_map/jit(_take)/gather | solution.py:71
  124.5 0.0 copy-done.8
  124.5 0.0 copy-start.16
  124.5 0.0 copy-start.17
  124.5 0.0 copy-start.20
  124.6 41.3 %all-gather.3.cloned.1.call-done = bf16[40960,128]{1,0:T(8,128)(2,1)} async-done(((bf16[5120,128]{1,0:T(8,128)(2,1)}), bf16[40960,128]{1,0:T(8,128)(2,1)}) %all-gather.3.cloned.1.call-update) | async-done | bytes 10485776 | tf_op jit(solution)/shard_map/all_gather | solution.py:66
  165.9 27.2 %gather_fusion.2 = bf16[8192,128]{1,0:T(8,128)(2,1)S(1)} fusion(bf16[40960,128]{1,0:T(8,128)(2,1)} %all-gather.3.cloned.1.call-done, s32[8192]{0:T(1024)S(1)} %fusion.22), kind=kCustom, calls=%fused_computation.2 | custom fusion | bytes 4227072 | tf_op jit(solution)/shard_map/jit(_take)/gather | solution.py:72
  193.1 0.0 copy-done.16
  193.1 0.0 copy-done.17
  193.1 0.0 copy-done.20
  193.1 10.4 %convolution_convert_fusion = bf16[8192,512]{1,0:T(8,128)(2,1)} fusion(bf16[128,512]{1,0:T(8,128)(2,1)S(1)} %copy-done.16, bf16[8192,512]{1,0:T(8,128)(2,1)} %param.24, bf16[512,128]{1,0:T(8,128)(2,1)S(1)} %copy-done.17, f32[8192,128]{1,0:T(8,128)} %gather_fusion.1, f32[128]{0:T(128)S(1)} %copy-done.20, bf16[8192,128]{1,0:T(8,128)(2,1)S(1)} %gather_fusion.2, ...), kind=kOutput, calls=%fused_computation.4 | convolution fusion | flops 2163212288 | bytes 23347712 | tf_op jit(solution)/shard_map/dot_general | solution.py:76
  203.5 11.8 %copy.24 = bf16[8192,512]{0,1:T(8,128)(2,1)} copy(bf16[8192,512]{1,0:T(8,128)(2,1)} %convolution_convert_fusion) | data formatting | bytes 16777216
  215.4 0.0 reduce-scatter.10.cloned.1.call-update
  215.4 0.0 copy-start.9
  215.4 0.0 copy-start.12
  215.4 0.0 copy-start.13
  215.4 0.0 reduce-scatter.8.cloned.1.call-start
  216.1 69.0 %reduce-scatter.10.cloned.1.call-done = bf16[128,8192]{1,0:T(8,128)(2,1)} async-done(((bf16[512,8192]{1,0:T(8,128)(2,1)}), bf16[128,8192]{1,0:T(8,128)(2,1)}) %reduce-scatter.10.cloned.1.call-update) | async-done | bytes 2097168
  285.1 3.2 copy.25
  288.4 0.0 copy-done.9
  288.4 0.0 copy-start.3
  288.4 2.2 fusion.4
  290.6 10.5 %all-reduce.1 = (bf16[8192]{0:T(1024)(128)(2,1)S(1)}, bf16[8192]{0:T(1024)(128)(2,1)S(1)}) all-reduce(bf16[8192]{0:T(1024)(128)(2,1)S(1)} %get-tuple-element.3, bf16[8192]{0:T(1024)(128)(2,1)S(1)} %get-tuple-element.2), channel_id=1, replica_groups=mesh['patch'=8,'hidden'=4] {'hidden'}, use_global_device_ids=true, to_apply=%region_4.5 | all-reduce | flops 16384 | bytes 65536 | tf_op jit(solution)/shard_map/psum | solution.py:22
  301.1 0.0 copy-done.12
  301.2 58.0 %scatter_custom_fusion = f32[40960,128]{1,0:T(8,128)} fusion(s32[8192]{0:T(1024)S(1)} %get-tuple-element.11, f32[]{:T(128)} %constant.43.clone.1, bf16[8192,128]{1,0:T(8,128)(2,1)S(1)} %copy.25, f32[8192]{0:T(1024)S(1)} %fusion.20, f32[128]{0:T(128)S(1)} %copy-done.12, f32[128]{0:T(128)S(1)} %copy-done.13, f32[8192]{0:T(1024)S(1)} %get-tuple-element.15, ...), kind=kCustom, calls=%fused_computation.5 | custom fusion | flops 8388608 | bytes 23168516 | tf_op jit(solution)/shard_map/scatter-add | solution.py:88
  359.1 12.0 %convert_element_type.69 = bf16[40960,128]{1,0:T(8,128)(2,1)} convert(f32[40960,128]{1,0:T(8,128)} %scatter_custom_fusion) | non-fusion elementwise | flops 5242880 | bytes 31457280 | tf_op jit(solution)/shard_map/convert_element_type | solution.py:90
  371.2 0.0 reduce-scatter.8.cloned.1.call-update
  371.2 0.0 all-gather.5.cloned.1.call-start
  371.3 178.8 %reduce-scatter.8.cloned.1.call-done = bf16[5120,128]{1,0:T(8,128)(2,1)} async-done(((bf16[40960,128]{1,0:T(8,128)(2,1)}), bf16[5120,128]{1,0:T(8,128)(2,1)}) %reduce-scatter.8.cloned.1.call-update) | async-done | bytes 1310736 | tf_op jit(solution)/shard_map/reduce_scatter | solution.py:89
  550.0 0.0 all-gather.5.cloned.1.call-update
  550.0 0.0 copy-start.18
  550.1 0.0 copy-start.19
  550.1 0.3 reduce-scatter.12.cloned.1.call-start
  550.4 4.0 convolution_add_fusion.2
  554.4 37.3 %all-gather.5.cloned.1.call-done = bf16[5120,512]{1,0:T(8,128)(2,1)} async-done(((bf16[5120,128]{1,0:T(8,128)(2,1)}), bf16[5120,512]{1,0:T(8,128)(2,1)}) %all-gather.5.cloned.1.call-update) | async-done | bytes 5242896 | tf_op jit(solution)/shard_map/all_gather | solution.py:93
  591.6 7.7 %convolution_convert_fusion.1 = bf16[5120,512]{1,0:T(8,128)(2,1)} fusion(bf16[128,512]{1,0:T(8,128)(2,1)S(1)} %copy-done.18, f32[5120,128]{1,0:T(8,128)S(1)} %convolution_add_fusion.2, bf16[5120,512]{1,0:T(8,128)(2,1)} %all-gather.5.cloned.1.call-done, bf16[512,128]{1,0:T(8,128)(2,1)S(1)} %copy-done.19), kind=kOutput, calls=%fused_computation.10 | convolution fusion | flops 1348730880 | bytes 13369344 | tf_op jit(solution)/shard_map/dot_general | solution.py:96
  599.4 7.9 %copy.26 = bf16[5120,512]{0,1:T(8,128)(2,1)} copy(bf16[5120,512]{1,0:T(8,128)(2,1)} %convolution_convert_fusion.1) | data formatting | bytes 10485760
  607.2 0.0 reduce-scatter.12.cloned.1.call-update
  607.3 0.0 copy-start.10
  607.3 0.0 copy-start.14
  607.3 0.0 copy-start.15
  607.3 0.0 copy-start.1
  607.3 9.6 %add_convert_fusion = bf16[8192,128]{1,0:T(8,128)(2,1)} fusion(bf16[8192,128]{1,0:T(8,128)(2,1)} %copy-done.3, bf16[8192,512]{1,0:T(8,128)(2,1)} %param.24, s32[]{:T(128)S(6)} %select_n.42, f32[8192]{0:T(1024)S(1)} %fusion.20, f32[128]{0:T(128)S(1)} %copy-done.12, f32[128]{0:T(128)S(1)} %copy-done.13, f32[8192]{0:T(1024)S(1)} %get-tuple-element.15, ...), kind=kLoop, calls=%fused_computation.14 | loop fusion | flops 10485760 | bytes 6391300 | tf_op jit(solution)/shard_map/convert_element_type | solution.py:87
  616.9 41.9 %reduce-scatter.12.cloned.1.call-done = bf16[128,5120]{1,0:T(8,128)(2,1)} async-done(((bf16[512,5120]{1,0:T(8,128)(2,1)}), bf16[128,5120]{1,0:T(8,128)(2,1)}) %reduce-scatter.12.cloned.1.call-update) | async-done | bytes 1310736
  658.8 2.4 copy.27
  661.2 2.7 fusion.5
  663.9 10.5 %all-reduce = (f32[5120]{0:T(1024)S(1)}, f32[5120]{0:T(1024)S(1)}) all-reduce(f32[5120]{0:T(1024)S(1)} %get-tuple-element.5, f32[5120]{0:T(1024)S(1)} %get-tuple-element.4), channel_id=1, replica_groups=mesh['patch'=8,'hidden'=4] {'hidden'}, use_global_device_ids=true, to_apply=%region_11.12 | all-reduce | flops 10240 | bytes 81920 | tf_op jit(solution)/shard_map/psum | solution.py:26
  674.5 5.0 add_convert_fusion.1
  (20 shorter events, 0.1 us)
Async XLA Ops:
  7.2 86.0 %copy-start = (bf16[3072,512]{1,0:T(8,128)(2,1)S(1)}, bf16[3072,512]{1,0:T(8,128)(2,1)}, u32[]{:S(2)}) copy-start(bf16[3072,512]{1,0:T(8,128)(2,1)} %param.22) | copy-start | bytes 9437188
  7.2 5.4 copy-start.7
  7.2 5.4 copy-start.2
  7.2 158.7 %all-gather.3.cloned.1.call-start = ((), (), s32[]{:S(2)}) async-start(), calls=%async_computation.3 | async-start | bytes 11796480 | tf_op jit(solution)/shard_map/all_gather | solution.py:66
  12.5 272.6 %reduce-scatter.10.cloned.1.call-start = ((), (), s32[]{:S(2)}) async-start(), calls=%async_computation.6 | async-start | bytes 10485760
  12.6 80.5 %copy-start.6 = (s32[8192]{0:T(1024)S(1)}, s32[8192]{0:T(1024)}, u32[]{:S(2)}) copy-start(s32[8192]{0:T(1024)} %param.25) | copy-start | bytes 98308
  12.6 80.6 %copy-start.4 = (bf16[512,128]{1,0:T(8,128)(2,1)S(1)}, bf16[512,128]{1,0:T(8,128)(2,1)}, u32[]{:S(2)}) copy-start(bf16[512,128]{1,0:T(8,128)(2,1)} %param.30) | copy-start | bytes 393220
  95.3 29.2 %copy-start.8 = (s32[8192]{0:T(1024)S(1)}, s32[8192]{0:T(1024)}, u32[]{:S(2)}) copy-start(s32[8192]{0:T(1024)} %gather_fusion) | copy-start | bytes 98308
  124.5 68.6 %copy-start.16 = (bf16[128,512]{1,0:T(8,128)(2,1)S(1)}, bf16[128,512]{1,0:T(8,128)(2,1)}, u32[]{:S(2)}) copy-start(bf16[128,512]{1,0:T(8,128)(2,1)} %param.33) | copy-start | bytes 393220
  124.5 68.6 %copy-start.17 = (bf16[512,128]{1,0:T(8,128)(2,1)S(1)}, bf16[512,128]{1,0:T(8,128)(2,1)}, u32[]{:S(2)}) copy-start(bf16[512,128]{1,0:T(8,128)(2,1)} %param.29) | copy-start | bytes 393220
  124.5 68.6 %copy-start.20 = (f32[128]{0:T(128)S(1)}, f32[128]{0:T(128)}, u32[]{:S(2)}) copy-start(f32[128]{0:T(128)} %param.32) | copy-start | bytes 1540
  215.4 73.0 %copy-start.9 = (f32[128]{0:T(128)S(1)}, f32[128]{0:T(128)}, u32[]{:S(2)}) copy-start(f32[128]{0:T(128)} %param.34) | copy-start | bytes 1540
  215.4 85.8 %copy-start.12 = (f32[128]{0:T(128)S(1)}, f32[128]{0:T(128)}, u32[]{:S(2)}) copy-start(f32[128]{0:T(128)} %param.36) | copy-start | bytes 1540
  215.4 85.8 %copy-start.13 = (f32[128]{0:T(128)S(1)}, f32[128]{0:T(128)}, u32[]{:S(2)}) copy-start(f32[128]{0:T(128)} %param.35) | copy-start | bytes 1540
  215.4 334.6 %reduce-scatter.8.cloned.1.call-start = ((), (), s32[]{:S(2)}) async-start(), calls=%async_computation.4 | async-start | bytes 11796480 | tf_op jit(solution)/shard_map/reduce_scatter | solution.py:89
  288.4 70.8 %copy-start.3 = (bf16[8192,128]{1,0:T(8,128)(2,1)}, bf16[8192,128]{1,0:T(8,128)(2,1)S(1)}, u32[]{:S(2)}) copy-start(bf16[8192,128]{1,0:T(8,128)(2,1)S(1)} %copy.25) | copy-start | bytes 6291460
  371.2 179.2 %copy-start.5 = (bf16[512,128]{1,0:T(8,128)(2,1)S(1)}, bf16[512,128]{1,0:T(8,128)(2,1)}, u32[]{:S(2)}) copy-start(bf16[512,128]{1,0:T(8,128)(2,1)} %param.37) | copy-start | bytes 393220
  371.2 179.2 %copy-start.11 = (f32[128]{0:T(128)S(1)}, f32[128]{0:T(128)}, u32[]{:S(2)}) copy-start(f32[128]{0:T(128)} %param.39) | copy-start | bytes 1540
  371.2 220.4 %all-gather.5.cloned.1.call-start = ((), (), s32[]{:S(2)}) async-start(), calls=%async_computation.5 | async-start | bytes 6553600 | tf_op jit(solution)/shard_map/all_gather | solution.py:93
  550.0 41.6 %copy-start.18 = (bf16[128,512]{1,0:T(8,128)(2,1)S(1)}, bf16[128,512]{1,0:T(8,128)(2,1)}, u32[]{:S(2)}) copy-start(bf16[128,512]{1,0:T(8,128)(2,1)} %param.40) | copy-start | bytes 393220
  550.1 41.6 %copy-start.19 = (bf16[512,128]{1,0:T(8,128)(2,1)S(1)}, bf16[512,128]{1,0:T(8,128)(2,1)}, u32[]{:S(2)}) copy-start(bf16[512,128]{1,0:T(8,128)(2,1)} %param.38) | copy-start | bytes 393220
  550.1 108.7 %reduce-scatter.12.cloned.1.call-start = ((), (), s32[]{:S(2)}) async-start(), calls=%async_computation.7 | async-start | bytes 6553600
  607.3 53.9 %copy-start.10 = (f32[128]{0:T(128)S(1)}, f32[128]{0:T(128)}, u32[]{:S(2)}) copy-start(f32[128]{0:T(128)} %param.41) | copy-start | bytes 1540
  607.3 67.2 %copy-start.14 = (f32[128]{0:T(128)S(1)}, f32[128]{0:T(128)}, u32[]{:S(2)}) copy-start(f32[128]{0:T(128)} %param.43) | copy-start | bytes 1540
  607.3 67.2 %copy-start.15 = (f32[128]{0:T(128)S(1)}, f32[128]{0:T(128)}, u32[]{:S(2)}) copy-start(f32[128]{0:T(128)} %param.42) | copy-start | bytes 1540
  607.3 72.2 %copy-start.1 = (bf16[3072,512]{1,0:T(8,128)(2,1)S(1)}, bf16[3072,512]{1,0:T(8,128)(2,1)}, u32[]{:S(2)}) copy-start(bf16[3072,512]{1,0:T(8,128)(2,1)} %param.22) | copy-start | bytes 9437188
Sparse Core Ops, SparseCore 0:
  12.6 153.2 all-gather.2
  215.5 69.5 reduce-scatter.9
  371.3 178.6 reduce-scatter.7
  551.4 40.1 all-gather.4
  607.4 51.3 reduce-scatter.11
where the time goes:
time: 687 us; the launch traced here: 686 us
  waiting for transfers between devices  368 us (54%)
  local copies, waits for them, and re-layouts  162 us (24%)
  other arithmetic  89.7 us (13%)
  matrix products  29.5 us (4%)
  blocking collectives  21 us (3%)
  between operations  14.8 us (2%)
    reduce_scatter x1, waiting for transfers between devices, shards(): lax.psum_scatter(spread_sums.astype(jnp.bfloat16), 'patch', scatter_dimen...  179 us
    unnamed x7, waiting for transfers between devices  111 us
    gather x1, local copies, waits for them, and re-layouts, shards(): target_rows = jnp.take(mesh_slot, receivers)  80.5 us
    scatter-add x1, other arithmetic, shards(): jax.ops.segment_sum(message, target_rows, num_segments=mesh_total)  58 us
    all_gather x1, waiting for transfers between devices, shards(): table = lax.all_gather(receiver_part, 'patch', axis=0, tiled=True)  41.3 us
    all_gather x1, waiting for transfers between devices, shards(): gathered = lax.all_gather(received, 'hidden', axis=1, tiled=True)  37.3 us
    gather x1, local copies, waits for them, and re-layouts, shards(): jnp.take(sender_part, sender_local, axis=0)  29.2 us
    gather x1, local copies, waits for them, and re-layouts, shards(): jnp.take(table, target_rows, axis=0).astype(jnp.float32)  27.2 us
  transfers between devices with their start and end apart: 5, of which 5 were waited for; matrix products, arithmetic and copies ran while one was open for 18% of the time, Pallas kernels for 0%

commit v1 on v0

v1 whole, which is shorter than its diff:
```python
import functools

import jax
import jax.numpy as jnp
from jax import lax
from jax.experimental import pallas as pl
from jax.experimental.pallas import tpu as pltpu
from jax.sharding import PartitionSpec as P

EPSILON = 1e-05
CHUNKS = 2


def row_block(rows, most):
    block = most
    while rows % block:
        block //= 2
    return block


def norm_own(total, gain, offset):
    width = total.shape[1]
    own = gain.shape[1]
    center = jnp.sum(total, axis=1, keepdims=True) / width
    centered = total - center
    spread = jnp.sum(centered * centered, axis=1, keepdims=True) / width
    return centered[:, :own] * lax.rsqrt(spread + EPSILON) * gain + offset


def own_columns(column, latent, own, block, first):
    if own % 128 == 0:
        return latent, pl.BlockSpec((block, own), lambda i, c: (i + first, c[0]))
    cut = lax.dynamic_slice_in_dim(latent, column[0] * own, own, 1)
    return cut, pl.BlockSpec((block, own), lambda i, c: (i + first, 0))


def edge_kernel(column, hidden_ref, latent_ref, live_ref, w_ref, bias_ref, gain_ref, shift_ref, message_ref, out_ref):
    total = jnp.dot(hidden_ref[...], w_ref[...], preferred_element_type=jnp.float32) + bias_ref[...]
    message = norm_own(total, gain_ref[...], shift_ref[...]) * live_ref[...]
    message_ref[...] = message
    out_ref[...] = (latent_ref[...].astype(jnp.float32) + message).astype(out_ref.dtype)


def edge_finish(column, hidden, latent, first_row, live, w_out, bias, gain, shift):
    rows, full = hidden.shape
    own = gain.shape[1]
    block = row_block(rows, 1024)
    first = first_row // block
    latent, latent_spec = own_columns(column, latent, own, block, first)
    return pl.pallas_call(
        edge_kernel,
        grid_spec=pltpu.PrefetchScalarGridSpec(
            num_scalar_prefetch=1,
            grid=(rows // block,),
            in_specs=[
                pl.BlockSpec((block, full), lambda i, c: (i, 0)),
                latent_spec,
                pl.BlockSpec((block, 1), lambda i, c: (i + first, 0)),
                pl.BlockSpec((full, full), lambda i, c: (0, 0)),
                pl.BlockSpec((1, full), lambda i, c: (0, 0)),
                pl.BlockSpec((1, own), lambda i, c: (0, 0)),
                pl.BlockSpec((1, own), lambda i, c: (0, 0)),
            ],
            out_specs=[
                pl.BlockSpec((block, own), lambda i, c: (i, 0)),
                pl.BlockSpec((block, own), lambda i, c: (i, 0)),
            ],
        ),
        out_shape=[
            jax.ShapeDtypeStruct((rows, own), jnp.float32),
            jax.ShapeDtypeStruct((rows, own), jnp.bfloat16),
        ],
        cost_estimate=pl.CostEstimate(
            flops=2 * rows * full * full, bytes_accessed=2 * rows * full + 8 * rows * own, transcendentals=0
        ),
        name="edge_finish",
    )(column, hidden, latent, live, w_out, bias, gain, shift)


def mesh_kernel(column, latent_ref, own_ref, summed_ref, w_in_ref, w_msg_ref, bias_in_ref, w_out_ref, bias_ref, gain_ref, shift_ref, out_ref):
    pre = jnp.dot(latent_ref[...], w_in_ref[...], preferred_element_type=jnp.float32)
    pre = pre + jnp.dot(summed_ref[...], w_msg_ref[...], preferred_element_type=jnp.float32) + bias_in_ref[...]
    hidden = jax.nn.silu(pre).astype(jnp.bfloat16)
    total = jnp.dot(hidden, w_out_ref[...], preferred_element_type=jnp.float32) + bias_ref[...]
    update = norm_own(total, gain_ref[...], shift_ref[...])
    out_ref[...] = (own_ref[...].astype(jnp.float32) + update).astype(out_ref.dtype)


def mesh_finish(column, latent, summed, w_in, w_msg, bias_in, w_out, bias, gain, shift):
    rows, full = latent.shape
    own = gain.shape[1]
    block = row_block(rows, 1024)
    whole = lambda i, c: (0, 0)
    own_latent, own_spec = own_columns(column, latent, own, block, 0)
    return pl.pallas_call(
        mesh_kernel,
        grid_spec=pltpu.PrefetchScalarGridSpec(
            num_scalar_prefetch=1,
            grid=(rows // block,),
            in_specs=[
                pl.BlockSpec((block, full), lambda i, c: (i, 0)),
                own_spec,
                pl.BlockSpec((block, full), lambda i, c: (i, 0)),
                pl.BlockSpec((full, full), whole),
                pl.BlockSpec((full, full), whole),
                pl.BlockSpec((1, full), whole),
                pl.BlockSpec((full, full), whole),
                pl.BlockSpec((1, full), whole),
                pl.BlockSpec((1, own), whole),
                pl.BlockSpec((1, own), whole),
            ],
            out_specs=pl.BlockSpec((block, own), lambda i, c: (i, 0)),
        ),
        out_shape=jax.ShapeDtypeStruct((rows, own), jnp.bfloat16),
        cost_estimate=pl.CostEstimate(
            flops=6 * rows * full * full, bytes_accessed=4 * rows * full + 4 * rows * own, transcendentals=rows * full
        ),
        name="mesh_finish",
    )(column, latent, own_latent, summed, w_in, w_msg, bias_in, w_out, bias, gain, shift)


def pieces(x, size):
    return [x] + [
        lax.ppermute(x, "hidden", [((j + k) % size, j) for j in range(size)]) for k in range(1, size)
    ]


def turned(x, shift, axis):
    return lax.dynamic_slice_in_dim(jnp.concatenate([x, x], axis), shift, x.shape[axis], axis)


def shards(
    hidden_size,
    grid_latent,
    mesh_latent,
    edge_latent,
    senders,
    receivers,
    mesh_slot,
    edge_counts,
    w_edge,
    w_sender,
    w_receiver,
    edge_bias,
    w_edge_out,
    edge_out_bias,
    edge_gain,
    edge_shift,
    w_mesh_in,
    w_message_in,
    mesh_bias,
    w_mesh_out,
    mesh_out_bias,
    mesh_gain,
    mesh_shift,
):
    patch_index = lax.axis_index("patch")
    column_index = lax.axis_index("hidden")
    own_grid = grid_latent.shape[0]
    own_edges = edge_latent.shape[0]
    width = w_edge.shape[1]
    full = w_edge.shape[0]
    mesh_total = mesh_slot.shape[0]
    column = jnp.reshape(column_index, (1,)).astype(jnp.int32)

    receiver_part = jnp.dot(mesh_latent, w_receiver, preferred_element_type=jnp.float32).astype(
        jnp.bfloat16
    )
    table = lax.all_gather(receiver_part, "patch", axis=0, tiled=True)

    outer = pieces(jnp.concatenate([w_edge_out, w_mesh_out], 0), hidden_size)
    inner = pieces(jnp.concatenate([w_mesh_in, w_message_in], 0), hidden_size)
    biases = jnp.concatenate(pieces(jnp.stack([edge_out_bias, mesh_bias, mesh_out_bias]), hidden_size), 1)
    to_first = lax.rem(hidden_size - column_index, hidden_size)
    edge_w_out = jnp.concatenate([part[:width] for part in outer], 0)
    edge_w_out = turned(turned(edge_w_out, to_first * width, 0), column_index * width, 1)
    mesh_w_out = turned(jnp.concatenate([part[width:] for part in outer], 0), column_index * width, 1)
    mesh_w_in = jnp.concatenate([part[:full] for part in inner], 1)
    mesh_w_msg = jnp.concatenate([part[full:] for part in inner], 1)

    target_rows = jnp.take(mesh_slot, receivers)
    sender_local = senders - patch_index * own_grid
    live = (jnp.arange(own_edges, dtype=jnp.int32) < edge_counts[0]).astype(jnp.float32)[:, None]
    sender_part = jnp.dot(grid_latent, w_sender, preferred_element_type=jnp.float32)
    sent = jnp.take(sender_part, sender_local, axis=0)

    step = own_edges // CHUNKS
    spread_sums = jnp.zeros((mesh_total, width), jnp.float32)
    edge_outs = []
    for at in range(0, own_edges, step):
        rows = slice(at, at + step)
        edge_pre = (
            jnp.dot(edge_latent[rows], w_edge, preferred_element_type=jnp.float32)
            + sent[rows]
            + jnp.take(table, target_rows[rows], axis=0).astype(jnp.float32)
            + edge_bias
        )
        edge_hidden = jax.nn.silu(edge_pre).astype(jnp.bfloat16)
        gathered_hidden = lax.all_gather(edge_hidden, "hidden", axis=1, tiled=True)
        message, edge_out = edge_finish(
            column,
            gathered_hidden,
            edge_latent,
            at,
            live,
            edge_w_out,
            biases[:1],
            edge_gain[None],
            edge_shift[None],
        )
        edge_outs.append(edge_out)
        spread_sums = spread_sums.at[target_rows[rows]].add(message)
    edge_out = jnp.concatenate(edge_outs, 0)

    received = lax.psum_scatter(
        spread_sums.astype(jnp.bfloat16), "patch", scatter_dimension=0, tiled=True
    )
    gathered = lax.all_gather(received, "hidden", axis=1, tiled=True)
    mesh_out = mesh_finish(
        column,
        mesh_latent,
        gathered,
        mesh_w_in,
        mesh_w_msg,
        biases[1:2],
        mesh_w_out,
        biases[2:3],
        mesh_gain[None],
        mesh_shift[None],
    )
    return (mesh_out, edge_out)


def solution(mesh):
    return jax.shard_map(
        functools.partial(shards, mesh.shape["hidden"]),
        mesh=mesh,
        in_specs=(
            P("patch", None),
            P("patch", None),
            P("patch", None),
            P("patch"),
            P("patch"),
            P(),
            P("patch"),
            P(None, "hidden"),
            P(None, "hidden"),
            P(None, "hidden"),
            P("hidden"),
            P("hidden", None),
            P("hidden"),
            P("hidden"),
            P("hidden"),
            P(None, "hidden"),
            P(None, "hidden"),
            P("hidden"),
            P("hidden", None),
            P("hidden"),
            P("hidden"),
            P("hidden"),
        ),
        out_specs=(P("patch", "hidden"), P("patch", "hidden")),
        check_vma=False,
    )
```

time: 687 us -> 571 us (0.83)
  waiting for transfers between devices: 368 us -> 299 us
  local copies, waits for them, and re-layouts: 162 us -> 109 us
  Pallas kernels: 0 us -> 29.5 us
  blocking collectives: 21 us -> 0 us
  matrix products: 29.5 us -> 16.1 us
  starting transfers between devices: 0.42 us -> 7.61 us
    unnamed x7 -> x5, waiting for transfers between devices: 111 us -> 0.08 us
    gather x1, local copies, waits for them, and re-layouts: 80.5 us -> 45.8 us  [shards(): target_rows = jnp.take(mesh_slot, receivers)]
    pallas_call x0 -> x3, Pallas kernels: none -> 29.5 us  [the longest x2 15.6 us: edge_finish(): pl.pallas_call(edge_kernel, grid_spec=pltpu.PrefetchScalarGridSpec(num_sc...]
    ppermute x0 -> x9, waiting for transfers between devices: none -> 29 us  [pieces(): lax.ppermute(x, 'hidden', [((j + k) % size, j) for j in range(size)])]
    all_gather x1, waiting for transfers between devices: 41.3 us -> 68 us  [shards(): table = lax.all_gather(receiver_part, 'patch', axis=0, tiled=True)]
    unnamed x46 -> x41, local copies, waits for them, and re-layouts: 25.5 us -> 0.15 us
    psum x2 -> x0, blocking collectives: 21 us -> none  [the longest x1 10.5 us: mesh_totals(): return lax.psum(values, 'hidden')]
    all_gather x1, waiting for transfers between devices: 37.3 us -> 22.2 us  [shards(): gathered = lax.all_gather(received, 'hidden', axis=1, tiled=True)]
  transfers between devices with their start and end apart: 5 -> 14, of which waited for: 5 -> 8; matrix products, arithmetic and copies ran while one was open for 18% -> 26% of each run, Pallas kernels for 0% -> 1%
where the time goes in v1:
time: 571 us; the launch traced here: 570 us
  waiting for transfers between devices  299 us (52%)
  local copies, waits for them, and re-layouts  109 us (19%)
  other arithmetic  94.5 us (17%)
  Pallas kernels  29.5 us (5%)
  matrix products  16.1 us (3%)
  between operations  14.8 us (3%)
  starting transfers between devices  7.61 us (1%)
    reduce_scatter x1, waiting for transfers between devices, shards(): lax.psum_scatter(spread_sums.astype(jnp.bfloat16), 'patch', scatter_dimen...  179 us
    all_gather x1, waiting for transfers between devices, shards(): table = lax.all_gather(receiver_part, 'patch', axis=0, tiled=True)  68 us
    scatter-add x2, other arithmetic, shards(): spread_sums = spread_sums.at[target_rows[rows]].add(message)  65.3 us
    gather x1, local copies, waits for them, and re-layouts, shards(): target_rows = jnp.take(mesh_slot, receivers)  45.8 us
    gather x2, local copies, waits for them, and re-layouts, shards(): jnp.take(table, target_rows[rows], axis=0).astype(jnp.float32)  32.7 us
    gather x1, local copies, waits for them, and re-layouts, shards(): sent = jnp.take(sender_part, sender_local, axis=0)  29.1 us
    ppermute x9, waiting for transfers between devices, pieces(): lax.ppermute(x, 'hidden', [((j + k) % size, j) for j in range(size)])  29 us
    all_gather x1, waiting for transfers between devices, shards(): gathered = lax.all_gather(received, 'hidden', axis=1, tiled=True)  22.2 us
  transfers between devices with their start and end apart: 14, of which 8 were waited for; matrix products, arithmetic and copies ran while one was open for 26% of the time, Pallas kernels for 1%

profile of v1, /device:TPU:0, one launch (start us, length us, event | category | flops | bytes accessed | tf_op | source)
XLA Modules:
  0.0 569.9 jit_solution(7473036390274413947)
XLA Ops:
  7.2 0.0 copy-start
  7.2 0.0 copy-start.11
  7.2 0.0 copy-start.10
  7.2 0.0 copy-start.2
  7.2 0.0 all-gather.5.cloned.1.call-start
  7.3 5.2 convolution_convert_fusion
  12.5 0.0 all-gather.5.cloned.1.call-update
  12.5 0.0 all-gather.7.cloned.1.call-start
  12.6 0.6 fusion.21
  13.2 45.8 %gather_fusion = s32[8192]{0:T(1024)S(1)} fusion(s32[40960]{0:T(1024)S(1)} %copy-done.2, s32[8192]{0:T(1024)} %get-tuple-element.34), kind=kCustom, calls=%fused_computation.2 | custom fusion | bytes 98304 | tf_op jit(solution)/shard_map/jit(_take)/gather | solution.py:181
  59.0 2.1 fusion.29
  61.2 29.1 %gather_fusion.1 = f32[8192,128]{1,0:T(8,128)} fusion(f32[3072,128]{1,0:T(8,128)} %fusion.29, s32[8192]{0:T(1024)S(1)} %copy-done.12), kind=kCustom, calls=%fused_computation.3 | custom fusion | bytes 8421376 | tf_op jit(solution)/shard_map/jit(_take)/gather | solution.py:185
  90.4 7.5 %broadcast_select_fusion = f32[8192,128]{1,0:T(8,128)} fusion(f32[8192,128]{1,0:T(8,128)} %gather_fusion.1, pred[8192]{0:T(1024)(128)(4,1)S(1)} %compare_and_fusion), kind=kLoop, calls=%fused_computation.22 | loop fusion | flops 1048576 | bytes 8396800 | tf_op jit(solution)/shard_map/jit(_take)/select_n | solution.py:185
  97.9 68.0 %all-gather.5.cloned.1.call-done = bf16[40960,128]{1,0:T(8,128)(2,1)} async-done(((bf16[5120,128]{1,0:T(8,128)(2,1)}), bf16[40960,128]{1,0:T(8,128)(2,1)}) %all-gather.5.cloned.1.call-update) | async-done | bytes 10485776 | tf_op jit(solution)/shard_map/all_gather | solution.py:169
  165.9 16.4 %gather_fusion.2 = bf16[4096,128]{1,0:T(8,128)(2,1)S(1)} fusion(bf16[40960,128]{1,0:T(8,128)(2,1)} %all-gather.5.cloned.1.call-done, s32[4096]{0:T(1024)S(1)} %get-tuple-element.28), kind=kCustom, calls=%fused_computation.clone | custom fusion | bytes 2113536 | tf_op jit(solution)/shard_map/jit(_take)/gather | solution.py:195
  182.3 0.0 copy-done.16
  182.3 4.3 multiply_convert_fusion.1
  186.6 0.0 all-gather.7.cloned.1.call-update
  186.7 0.0 all-gather.9.cloned.1.call-start
  186.7 16.4 %gather_fusion.3 = bf16[4096,128]{1,0:T(8,128)(2,1)S(1)} fusion(bf16[40960,128]{1,0:T(8,128)(2,1)} %all-gather.5.cloned.1.call-done, s32[4096]{0:T(1024)S(1)} %get-tuple-element.27), kind=kCustom, calls=%fused_computation.1.clone | custom fusion | bytes 2113536 | tf_op jit(solution)/shard_map/jit(_take)/gather | solution.py:195
  203.1 0.0 copy-start.5
  203.1 0.0 copy-start.8
  203.1 0.0 copy-start.13
  203.1 0.0 copy-start.14
  203.1 0.0 copy-start.15
  203.1 4.4 multiply_convert_fusion
  207.6 0.0 all-gather.9.cloned.1.call-update
  207.6 0.0 reduce-scatter.2.cloned.1.call-start
  207.7 0.2 collective-permute-start
  208.0 1.4 collective-permute-start.1
  209.3 0.4 collective-permute-start.3
  209.7 1.5 collective-permute-start.4
  211.2 0.0 collective-permute-start.5
  211.8 2.5 fusion.8.live_ref
  214.3 9.9 %collective-permute-done.3 = f32[3,128]{1,0:T(4,128)S(1)} collective-permute-done((f32[3,128]{1,0:T(4,128)S(1)}, f32[3,128]{1,0:T(4,128)S(1)}, u32[]{:S(2)}, u32[]{:S(2)}) %collective-permute-start.3) | collective-permute-done | bytes 1568 | tf_op jit(solution)/shard_map/ppermute | solution.py:124
  224.2 2.2 collective-permute-start.2
  226.4 0.0 collective-permute-done.4
  226.4 0.0 collective-permute-done.5
  226.4 0.6 pad_maximum_fusion.3
  227.0 0.0 collective-permute-done
  227.1 0.0 collective-permute-done.1
  227.1 3.3 collective-permute-done.2
  230.4 0.7 fusion.23
  231.2 1.0 fusion.20.w_ref
  232.2 7.9 %edge_finish.2 = (f32[4096,128]{1,0:T(8,128)}, bf16[4096,128]{1,0:T(8,128)(2,1)}) custom-call(s32[1]{0:T(128)} %bitcast.column, bf16[4096,512]{1,0:T(8,128)(2,1)} %all-gather.7.cloned.1.call-done.hidden_ref, bf16[8192,512]{1,0:T(8,128)(2,1)} %latent_ref.4, f32[8192,1]{1,0:T(8,128)} %fusion.8.live_ref, bf16[512,512]{1,0:T(8,128)(2,1)} %fusion.20.w_ref, ...), custom_call_target="tpu_custom_call" | custom-call | flops 2147483648 | bytes 8388608 | tf_op jit(solution)/shard_map/edge_finish/pallas_call | solution.py:50
  240.1 30.9 %scatter_custom_fusion = f32[40960,128]{1,0:T(8,128)} fusion(s32[4096]{0:T(1024)S(1)} %get-tuple-element.30, f32[4096,128]{1,0:T(8,128)} %get-tuple-element.7, f32[]{:T(128)} %constant.36.clone.1), kind=kCustom, calls=%fused_computation.6 | custom fusion | flops 524288 | bytes 20972032 | tf_op jit(solution)/shard_map/scatter-add | solution.py:212
  271.1 7.7 %edge_finish.3 = (f32[4096,128]{1,0:T(8,128)}, bf16[4096,128]{1,0:T(8,128)(2,1)}) custom-call(s32[1]{0:T(128)} %bitcast.column, bf16[4096,512]{1,0:T(8,128)(2,1)} %all-gather.9.cloned.1.call-done.hidden_ref, bf16[8192,512]{1,0:T(8,128)(2,1)} %latent_ref.4, f32[8192,1]{1,0:T(8,128)} %fusion.8.live_ref, bf16[512,512]{1,0:T(8,128)(2,1)} %fusion.20.w_ref, ...), custom_call_target="tpu_custom_call" | custom-call | flops 2147483648 | bytes 8388608 | tf_op jit(solution)/shard_map/edge_finish/pallas_call | solution.py:50
  278.8 34.3 %scatter_fusion = f32[40960,128]{1,0:T(8,128)} fusion(f32[40960,128]{1,0:T(8,128)} %scatter_custom_fusion, s32[4096]{0:T(1024)S(1)} %get-tuple-element.29, f32[4096,128]{1,0:T(8,128)} %get-tuple-element.8), kind=kCustom, calls=%fused_computation.5 | custom fusion | flops 524288 | bytes 6307840 | tf_op jit(solution)/shard_map/scatter-add | solution.py:212
  313.1 12.0 %convert_element_type.34 = bf16[40960,128]{1,0:T(8,128)(2,1)} convert(f32[40960,128]{1,0:T(8,128)} %scatter_fusion) | non-fusion elementwise | flops 5242880 | bytes 31457280 | tf_op jit(solution)/shard_map/convert_element_type | solution.py:216
  325.1 0.0 reduce-scatter.2.cloned.1.call-update
  325.2 0.0 all-gather.11.cloned.1.call-start
  325.2 179.4 %reduce-scatter.2.cloned.1.call-done = bf16[5120,128]{1,0:T(8,128)(2,1)} async-done(((bf16[40960,128]{1,0:T(8,128)(2,1)}), bf16[5120,128]{1,0:T(8,128)(2,1)}) %reduce-scatter.2.cloned.1.call-update) | async-done | bytes 1310736 | tf_op jit(solution)/shard_map/reduce_scatter | solution.py:215
  504.6 0.0 all-gather.11.cloned.1.call-update
  504.7 0.9 collective-permute-start.6
  505.6 0.7 collective-permute-start.7
  506.3 0.2 collective-permute-start.8
  506.5 5.7 collective-permute-done.6
  512.2 9.8 %collective-permute-done.7 = bf16[1024,128]{1,0:T(8,128)(2,1)S(1)} collective-permute-done((bf16[1024,128]{1,0:T(8,128)(2,1)S(1)}, bf16[1024,128]{1,0:T(8,128)(2,1)S(1)}, u32[]{:S(2)}, u32[]{:S(2)}) %collective-permute-start.7) | collective-permute-done | bytes 262176 | tf_op jit(solution)/shard_map/ppermute | solution.py:124
  522.0 0.3 collective-permute-done.8
  522.3 1.1 pad_maximum_fusion.1
  523.4 2.4 fusion.16.w_out_ref
  525.8 1.5 pad_maximum_fusion
  527.3 22.2 %all-gather.11.cloned.1.call-done.summed_ref = bf16[5120,512]{1,0:T(8,128)(2,1)} async-done(((bf16[5120,128]{1,0:T(8,128)(2,1)}), bf16[5120,512]{1,0:T(8,128)(2,1)}) %all-gather.11.cloned.1.call-update) | async-done | bytes 5242896 | tf_op jit(solution)/shard_map/all_gather | solution.py:218
  549.5 13.8 %mesh_finish.1 = bf16[5120,128]{1,0:T(8,128)(2,1)} custom-call(s32[1]{0:T(128)} %bitcast.column, bf16[5120,512]{1,0:T(8,128)(2,1)} %own_ref.1, bf16[5120,512]{1,0:T(8,128)(2,1)} %own_ref.1, bf16[5120,512]{1,0:T(8,128)(2,1)} %all-gather.11.cloned.1.call-done.summed_ref, bf16[512,512]{1,0:T(8,128)(2,1)} %get-tuple-element.36.w_in_ref, ...), custom_call_target="tpu_custom_call" | custom-call | flops 8053063680 | bytes 13107200 | tf_op jit(solution)/shard_map/mesh_finish/pallas_call | solution.py:95
  (47 shorter events, 0.4 us)
Async XLA Ops:
  7.2 51.8 %copy-start = (bf16[3072,512]{1,0:T(8,128)(2,1)S(1)}, bf16[3072,512]{1,0:T(8,128)(2,1)}, u32[]{:S(2)}) copy-start(bf16[3072,512]{1,0:T(8,128)(2,1)} %param.24) | copy-start | bytes 9437188
  7.2 5.4 copy-start.11
  7.2 5.4 copy-start.10
  7.2 6.0 %copy-start.2 = (s32[40960]{0:T(1024)S(1)}, s32[40960]{0:T(1024)}, u32[]{:S(2)}) copy-start(s32[40960]{0:T(1024)} %param.29) | copy-start | bytes 491524
  7.2 158.7 %all-gather.5.cloned.1.call-start = ((), (), s32[]{:S(2)}) async-start(), calls=%async_computation.1 | async-start | bytes 11796480 | tf_op jit(solution)/shard_map/all_gather | solution.py:169
  12.5 219.7 %all-gather.7.cloned.1.call-start = ((), (), s32[]{:S(2)}) async-start(), calls=%async_computation.2 | async-start | bytes 5242880 | tf_op jit(solution)/shard_map/all_gather | solution.py:199
  13.2 45.8 %copy-start.9 = (bf16[512,128]{1,0:T(8,128)(2,1)S(1)}, bf16[512,128]{1,0:T(8,128)(2,1)}, u32[]{:S(2)}) copy-start(bf16[512,128]{1,0:T(8,128)(2,1)} %param.32) | copy-start | bytes 393220
  59.0 2.1 copy-start.12
  165.9 16.4 %copy-start.16 = (bf16[512,128]{1,0:T(8,128)(2,1)S(1)}, bf16[512,128]{1,0:T(8,128)(2,1)}, u32[]{:S(2)}) copy-start(bf16[512,128]{1,0:T(8,128)(2,1)} %param.31) | copy-start | bytes 393220
  165.9 16.4 %copy-start.17 = (f32[128]{0:T(128)S(1)}, f32[128]{0:T(128)}, u32[]{:S(2)}) copy-start(f32[128]{0:T(128)} %param.34) | copy-start | bytes 1540
  186.7 84.4 %all-gather.9.cloned.1.call-start = ((), (), s32[]{:S(2)}) async-start(), calls=%async_computation.3 | async-start | bytes 5242880 | tf_op jit(solution)/shard_map/all_gather | solution.py:199
  203.1 4.6 copy-start.5
  203.1 4.6 copy-start.8
  203.1 6.2 %copy-start.13 = (f32[128]{0:T(128)S(1)}, f32[128]{0:T(128)}, u32[]{:S(2)}) copy-start(f32[128]{0:T(128)} %param.43) | copy-start | bytes 1540
  203.1 6.2 %copy-start.14 = (f32[128]{0:T(128)S(1)}, f32[128]{0:T(128)}, u32[]{:S(2)}) copy-start(f32[128]{0:T(128)} %param.41) | copy-start | bytes 1540
  203.1 6.2 %copy-start.15 = (f32[128]{0:T(128)S(1)}, f32[128]{0:T(128)}, u32[]{:S(2)}) copy-start(f32[128]{0:T(128)} %param.36) | copy-start | bytes 1540
  207.6 297.0 %reduce-scatter.2.cloned.1.call-start = ((), (), s32[]{:S(2)}) async-start(), calls=%async_computation.4 | async-start | bytes 11796480 | tf_op jit(solution)/shard_map/reduce_scatter | solution.py:215
  207.7 19.3 %collective-permute-start = (bf16[256,512]{1,0:T(8,128)(2,1)S(1)}, bf16[256,512]{1,0:T(8,128)(2,1)S(1)}, u32[]{:S(2)}, u32[]{:S(2)}) collective-permute-start(bf16[256,512]{1,0:T(8,128)(2,1)S(1)} %constant_dynamic-update-slice_fusion), channel_id=1, source_target_pairs={{1,0},{2,1},{3,2},{0,3},{5,4},{6,5},{7,6},{4,7},{9,8},{10,9},{11,1... | collective-permute-start | bytes 786440 | tf_op jit(solution)/shard_map/ppermute | solution.py:124
  208.0 19.1 %collective-permute-start.1 = (bf16[256,512]{1,0:T(8,128)(2,1)S(1)}, bf16[256,512]{1,0:T(8,128)(2,1)S(1)}, u32[]{:S(2)}, u32[]{:S(2)}) collective-permute-start(bf16[256,512]{1,0:T(8,128)(2,1)S(1)} %constant_dynamic-update-slice_fusion), channel_id=1, source_target_pairs={{2,0},{3,1},{0,2},{1,3},{6,4},{7,5},{4,6},{5,7},{10,8},{11,9},{8,1... | collective-permute-start | bytes 786440 | tf_op jit(solution)/shard_map/ppermute | solution.py:124
  209.3 14.9 %collective-permute-start.3 = (f32[3,128]{1,0:T(4,128)S(1)}, f32[3,128]{1,0:T(4,128)S(1)}, u32[]{:S(2)}, u32[]{:S(2)}) collective-permute-start(f32[3,128]{1,0:T(4,128)S(1)} %pad_maximum_fusion.10), channel_id=1, source_target_pairs={{1,0},{2,1},{3,2},{0,3},{5,4},{6,5},{7,6},{4,7},{9,8},{10,9},{11,1... | collective-permute-start | bytes 4616 | tf_op jit(solution)/shard_map/ppermute | solution.py:124
  209.7 16.7 %collective-permute-start.4 = (f32[3,128]{1,0:T(4,128)S(1)}, f32[3,128]{1,0:T(4,128)S(1)}, u32[]{:S(2)}, u32[]{:S(2)}) collective-permute-start(f32[3,128]{1,0:T(4,128)S(1)} %pad_maximum_fusion.10), channel_id=1, source_target_pairs={{2,0},{3,1},{0,2},{1,3},{6,4},{7,5},{4,6},{5,7},{10,8},{11,9},{8,1... | collective-permute-start | bytes 4616 | tf_op jit(solution)/shard_map/ppermute | solution.py:124
  211.2 15.3 %collective-permute-start.5 = (f32[3,128]{1,0:T(4,128)S(1)}, f32[3,128]{1,0:T(4,128)S(1)}, u32[]{:S(2)}, u32[]{:S(2)}) collective-permute-start(f32[3,128]{1,0:T(4,128)S(1)} %pad_maximum_fusion.10), channel_id=1, source_target_pairs={{3,0},{0,1},{1,2},{2,3},{7,4},{4,5},{5,6},{6,7},{11,8},{8,9},{9,10... | collective-permute-start | bytes 4616 | tf_op jit(solution)/shard_map/ppermute | solution.py:124
  224.2 6.2 %collective-permute-start.2 = (bf16[256,512]{1,0:T(8,128)(2,1)S(1)}, bf16[256,512]{1,0:T(8,128)(2,1)S(1)}, u32[]{:S(2)}, u32[]{:S(2)}) collective-permute-start(bf16[256,512]{1,0:T(8,128)(2,1)S(1)} %constant_dynamic-update-slice_fusion), channel_id=1, source_target_pairs={{3,0},{0,1},{1,2},{2,3},{7,4},{4,5},{5,6},{6,7},{11,8},{8,9},{9,10... | collective-permute-start | bytes 786440 | tf_op jit(solution)/shard_map/ppermute | solution.py:124
  325.1 179.5 %copy-start.6 = (bf16[512,128]{1,0:T(8,128)(2,1)S(1)}, bf16[512,128]{1,0:T(8,128)(2,1)}, u32[]{:S(2)}) copy-start(bf16[512,128]{1,0:T(8,128)(2,1)} %param.39) | copy-start | bytes 393220
  325.1 179.6 %copy-start.7 = (bf16[512,128]{1,0:T(8,128)(2,1)S(1)}, bf16[512,128]{1,0:T(8,128)(2,1)}, u32[]{:S(2)}) copy-start(bf16[512,128]{1,0:T(8,128)(2,1)} %param.40) | copy-start | bytes 393220
  325.2 224.3 %all-gather.11.cloned.1.call-start = ((), (), s32[]{:S(2)}) async-start(), calls=%async_computation.5 | async-start | bytes 6553600 | tf_op jit(solution)/shard_map/all_gather | solution.py:218
  504.6 21.2 %copy-start.3 = (bf16[4096,128]{1,0:T(8,128)(2,1)S(1)}, bf16[4096,128]{1,0:T(8,128)(2,1)}, u32[]{:S(2)}) copy-start(bf16[4096,128]{1,0:T(8,128)(2,1)} %get-tuple-element.9) | copy-start | bytes 3145732
  504.6 21.2 %copy-start.4 = (bf16[4096,128]{1,0:T(8,128)(2,1)S(1)}, bf16[4096,128]{1,0:T(8,128)(2,1)}, u32[]{:S(2)}) copy-start(bf16[4096,128]{1,0:T(8,128)(2,1)} %get-tuple-element.10) | copy-start | bytes 3145732
  504.7 7.4 %collective-permute-start.6 = (bf16[1024,128]{1,0:T(8,128)(2,1)S(1)}, bf16[1024,128]{1,0:T(8,128)(2,1)S(1)}, u32[]{:S(2)}, u32[]{:S(2)}) collective-permute-start(bf16[1024,128]{1,0:T(8,128)(2,1)S(1)} %constant_dynamic-update-slice_fusion.4), channel_id=1, source_target_pairs={{1,0},{2,1},{3,2},{0,3},{5,4},{6,5},{7,6},{4,7},{9,8},{10,9},{11,1... | collective-permute-start | bytes 786440 | tf_op jit(solution)/shard_map/ppermute | solution.py:124
  505.6 16.4 %collective-permute-start.7 = (bf16[1024,128]{1,0:T(8,128)(2,1)S(1)}, bf16[1024,128]{1,0:T(8,128)(2,1)S(1)}, u32[]{:S(2)}, u32[]{:S(2)}) collective-permute-start(bf16[1024,128]{1,0:T(8,128)(2,1)S(1)} %constant_dynamic-update-slice_fusion.4), channel_id=1, source_target_pairs={{2,0},{3,1},{0,2},{1,3},{6,4},{7,5},{4,6},{5,7},{10,8},{11,9},{8,1... | collective-permute-start | bytes 786440 | tf_op jit(solution)/shard_map/ppermute | solution.py:124
  506.3 16.0 %collective-permute-start.8 = (bf16[1024,128]{1,0:T(8,128)(2,1)S(1)}, bf16[1024,128]{1,0:T(8,128)(2,1)S(1)}, u32[]{:S(2)}, u32[]{:S(2)}) collective-permute-start(bf16[1024,128]{1,0:T(8,128)(2,1)S(1)} %constant_dynamic-update-slice_fusion.4), channel_id=1, source_target_pairs={{3,0},{0,1},{1,2},{2,3},{7,4},{4,5},{5,6},{6,7},{11,8},{8,9},{9,10... | collective-permute-start | bytes 786440 | tf_op jit(solution)/shard_map/ppermute | solution.py:124
  549.5 13.8 %copy-start.1 = (bf16[3072,512]{1,0:T(8,128)(2,1)S(1)}, bf16[3072,512]{1,0:T(8,128)(2,1)}, u32[]{:S(2)}) copy-start(bf16[3072,512]{1,0:T(8,128)(2,1)} %param.24) | copy-start | bytes 9437188
Sparse Core Ops, SparseCore 0:
  12.6 153.2 all-gather.4
  186.8 39.6 all-gather.6
  228.0 36.7 all-gather.8
  325.3 179.3 reduce-scatter.1
  506.0 43.3 all-gather.10

commit v2 on v1

--- a/solution.py
+++ b/solution.py
@@ -79,7 +79,8 @@
 
 def mesh_kernel(column, latent_ref, own_ref, summed_ref, w_in_ref, w_msg_ref, bias_in_ref, w_out_ref, bias_ref, gain_ref, shift_ref, out_ref):
     pre = jnp.dot(latent_ref[...], w_in_ref[...], preferred_element_type=jnp.float32)
-    pre = pre + jnp.dot(summed_ref[...], w_msg_ref[...], preferred_element_type=jnp.float32) + bias_in_ref[...]
+    summed = jnp.concatenate([summed_ref[h] for h in range(summed_ref.shape[0])], axis=1)
+    pre = pre + jnp.dot(summed, w_msg_ref[...], preferred_element_type=jnp.float32) + bias_in_ref[...]
     hidden = jax.nn.silu(pre).astype(jnp.bfloat16)
     total = jnp.dot(hidden, w_out_ref[...], preferred_element_type=jnp.float32) + bias_ref[...]
     update = norm_own(total, gain_ref[...], shift_ref[...])
@@ -100,7 +101,7 @@
             in_specs=[
                 pl.BlockSpec((block, full), lambda i, c: (i, 0)),
                 own_spec,
-                pl.BlockSpec((block, full), lambda i, c: (i, 0)),
+                pl.BlockSpec((summed.shape[0], block, summed.shape[2]), lambda i, c: (0, i, 0)),
                 pl.BlockSpec((full, full), whole),
                 pl.BlockSpec((full, full), whole),
                 pl.BlockSpec((1, full), whole),
@@ -119,17 +120,190 @@
     )(column, latent, own_latent, summed, w_in, w_msg, bias_in, w_out, bias, gain, shift)
 
 
+def combine_kernel(sizes, part_ref, out_ref, own, paired, crossed, gathered, own_sem, pair_send, pair_recv, cross_send, cross_recv, side_send, side_recv, far_send, far_recv, relay_send, relay_recv, out_sem):
+    outer_size, far_size, chunks, rows = sizes
+    patch, rank = lax.axis_index("patch"), lax.axis_index("hidden")
+    outer, inner = patch // 2, patch % 2
+    far, side = rank // 2, rank % 2
+    pair_peer = outer * 2 + (1 - inner)
+    side_peer = far * 2 + (1 - side)
+    shift = lambda at, by, size: lax.rem(at + by, size)
+    cross_peers = [shift(outer, k + 1, outer_size) * 2 + inner for k in range(outer_size - 1)]
+    far_peers = [shift(far, k + 1, far_size) * 2 + side for k in range(far_size - 1)]
+    blocks = [shift(outer, k + 1, outer_size) for k in range(outer_size)]
+
+    barrier = pltpu.get_barrier_semaphore()
+    for peer in [pair_peer] + cross_peers:
+        pl.semaphore_signal(barrier, inc=1, device_id={"patch": peer}, device_id_type=pl.DeviceIdType.MESH)
+    for peer in [side_peer] + far_peers:
+        pl.semaphore_signal(barrier, inc=1, device_id={"hidden": peer}, device_id_type=pl.DeviceIdType.MESH)
+    pl.semaphore_wait(barrier, outer_size + far_size)
+
+    def send(src, dst, send_sem, recv_sem, axis, peer):
+        copy = pltpu.make_async_remote_copy(
+            src_ref=src,
+            dst_ref=dst,
+            send_sem=send_sem,
+            recv_sem=recv_sem,
+            device_id={axis: peer},
+            device_id_type=pl.DeviceIdType.MESH,
+        )
+        copy.start()
+        return copy
+
+    def span(c):
+        return pl.ds(c * rows, rows)
+
+    loads, pairs, crosses, sides, fars, relays, outs = [], {}, {}, {}, {}, {}, []
+    for c in range(chunks):
+        load = pltpu.make_async_copy(part_ref.at[:, inner, span(c)], own.at[c], own_sem.at[c])
+        load.start()
+        loads.append(load)
+        for k in range(outer_size):
+            pairs[c, k] = send(
+                part_ref.at[blocks[k], 1 - inner, span(c)],
+                paired.at[c, k],
+                pair_send.at[c, k],
+                pair_recv.at[c, k],
+                "patch",
+                pair_peer,
+            )
+
+    tile = row_block(rows, 128)
+
+    def reduce_pair(c):
+        loads[c].wait()
+        for k in range(outer_size - 1):
+            pairs[c, k].wait_recv()
+
+            def add(i, carry):
+                at = pl.ds(pl.multiple_of(i * tile, tile), tile)
+                total = own[c, blocks[k], at].astype(jnp.float32) + paired[c, k, at].astype(jnp.float32)
+                own[c, blocks[k], at] = total.astype(jnp.bfloat16)
+                return carry
+
+            lax.fori_loop(0, rows // tile, add, 0)
+            crosses[c, k] = send(
+                own.at[c, blocks[k]],
+                crossed.at[c, k],
+                cross_send.at[c, k],
+                cross_recv.at[c, k],
+                "patch",
+                cross_peers[k],
+            )
+        pairs[c, outer_size - 1].wait_recv()
+
+    def emit(c, source, sem):
+        copy = pltpu.make_async_copy(gathered.at[c, source], out_ref.at[source, span(c)], sem)
+        copy.start()
+        outs.append(copy)
+
+    def finish(c):
+        for k in range(outer_size - 1):
+            crosses[c, k].wait_recv()
+
+        def add(i, carry):
+            at = pl.ds(pl.multiple_of(i * tile, tile), tile)
+            total = own[c, outer, at].astype(jnp.float32) + paired[c, outer_size - 1, at].astype(jnp.float32)
+            for k in range(outer_size - 1):
+                total = total + crossed[c, k, at].astype(jnp.float32)
+            gathered[c, rank, at] = total.astype(jnp.bfloat16)
+            return carry
+
+        lax.fori_loop(0, rows // tile, add, 0)
+        mine = gathered.at[c, rank]
+        for k in range(far_size - 1):
+            fars[c, k] = send(mine, mine, far_send.at[c, k], far_recv.at[c, k], "hidden", far_peers[k])
+        sides[c] = send(mine, mine, side_send.at[c], side_recv.at[c], "hidden", side_peer)
+        emit(c, rank, out_sem.at[c, 0])
+
+    def relay(c):
+        for k in range(far_size - 1):
+            fars[c, k].wait_recv()
+            source = shift(far, far_size - 1 - k, far_size) * 2 + side
+            block = gathered.at[c, source]
+            relays[c, k] = send(block, block, relay_send.at[c, k], relay_recv.at[c, k], "hidden", side_peer)
+            emit(c, source, out_sem.at[c, 1 + k])
+
+    def collect(c):
+        sides[c].wait_recv()
+        emit(c, side_peer, out_sem.at[c, far_size])
+        for k in range(far_size - 1):
+            relays[c, k].wait_recv()
+            source = shift(far, far_size - 1 - k, far_size) * 2 + (1 - side)
+            emit(c, source, out_sem.at[c, far_size + 1 + k])
+
+    for c in range(chunks + 3):
+        if c < chunks:
+            reduce_pair(c)
+        if 0 <= c - 1 < chunks:
+            finish(c - 1)
+        if 0 <= c - 2 < chunks:
+            relay(c - 2)
+        if 0 <= c - 3 < chunks:
+            collect(c - 3)
+    for group in (pairs, crosses, sides, fars, relays):
+        for copy in group.values():
+            copy.wait_send()
+    for copy in outs:
+        copy.wait()
+
+
+def combine(parts, patches, ranks):
+    total_rows, width = parts.shape
+    rows = total_rows // patches
+    outer_size, far_size = patches // 2, ranks // 2
+    chunks = 5 if rows % 80 == 0 else 4
+    size = rows // chunks
+    dma = pltpu.SemaphoreType.DMA
+    cross = (chunks, outer_size - 1)
+    far = (chunks, far_size - 1)
+    return pl.pallas_call(
+        functools.partial(combine_kernel, (outer_size, far_size, chunks, size)),
+        in_specs=[pl.BlockSpec(memory_space=pl.ANY)],
+        out_specs=pl.BlockSpec(memory_space=pl.ANY),
+        out_shape=jax.ShapeDtypeStruct((ranks, rows, width), jnp.bfloat16),
+        scratch_shapes=[
+            pltpu.VMEM((chunks, outer_size, size, width), jnp.bfloat16),
+            pltpu.VMEM((chunks, outer_size, size, width), jnp.bfloat16),
+            pltpu.VMEM(cross + (size, width), jnp.bfloat16),
+            pltpu.VMEM((chunks, ranks, size, width), jnp.bfloat16),
+            dma((chunks,)),
+            dma((chunks, outer_size)),
+            dma((chunks, outer_size)),
+            dma(cross),
+            dma(cross),
+            dma((chunks,)),
+            dma((chunks,)),
+            dma(far),
+            dma(far),
+            dma(far),
+            dma(far),
+            dma((chunks, ranks)),
+        ],
+        compiler_params=pltpu.CompilerParams(
+            collective_id=0, has_side_effects=True, vmem_limit_bytes=48 * 1024 * 1024
+        ),
+        name="combine",
+    )(parts.reshape(outer_size, 2, rows, width))
+
+
 def pieces(x, size):
     return [x] + [
         lax.ppermute(x, "hidden", [((j + k) % size, j) for j in range(size)]) for k in range(1, size)
     ]
 
 
+def rows_at(x, index):
+    return x.at[index].get(mode="promise_in_bounds")
+
+
 def turned(x, shift, axis):
     return lax.dynamic_slice_in_dim(jnp.concatenate([x, x], axis), shift, x.shape[axis], axis)
 
 
 def shards(
+    patches,
     hidden_size,
     grid_latent,
     mesh_latent,
@@ -178,11 +352,14 @@
     mesh_w_in = jnp.concatenate([part[:full] for part in inner], 1)
     mesh_w_msg = jnp.concatenate([part[full:] for part in inner], 1)
 
-    target_rows = jnp.take(mesh_slot, receivers)
+    target_rows = rows_at(mesh_slot, receivers)
+    weights = (edge_w_out, mesh_w_out, mesh_w_in, mesh_w_msg, biases)
+    target_rows, weights = lax.optimization_barrier((target_rows, weights))
+    edge_w_out, mesh_w_out, mesh_w_in, mesh_w_msg, biases = weights
     sender_local = senders - patch_index * own_grid
     live = (jnp.arange(own_edges, dtype=jnp.int32) < edge_counts[0]).astype(jnp.float32)[:, None]
     sender_part = jnp.dot(grid_latent, w_sender, preferred_element_type=jnp.float32)
-    sent = jnp.take(sender_part, sender_local, axis=0)
+    sent = rows_at(sender_part, sender_local)
 
     step = own_edges // CHUNKS
     spread_sums = jnp.zeros((mesh_total, width), jnp.float32)
@@ -192,7 +369,7 @@
         edge_pre = (
             jnp.dot(edge_latent[rows], w_edge, preferred_element_type=jnp.float32)
             + sent[rows]
-            + jnp.take(table, target_rows[rows], axis=0).astype(jnp.float32)
+            + rows_at(table, target_rows[rows]).astype(jnp.float32)
             + edge_bias
         )
         edge_hidden = jax.nn.silu(edge_pre).astype(jnp.bfloat16)
@@ -209,13 +386,15 @@
             edge_shift[None],
         )
         edge_outs.append(edge_out)
-        spread_sums = spread_sums.at[target_rows[rows]].add(message)
+        spread_sums = spread_sums.at[target_rows[rows]].add(message, mode="promise_in_bounds")
     edge_out = jnp.concatenate(edge_outs, 0)
 
-    received = lax.psum_scatter(
-        spread_sums.astype(jnp.bfloat16), "patch", scatter_dimension=0, tiled=True
-    )
-    gathered = lax.all_gather(received, "hidden", axis=1, tiled=True)
+    spread_sums = spread_sums.astype(jnp.bfloat16)
+    if width % 128 == 0 and patches % 2 == 0 and patches > 2 and hidden_size % 2 == 0 and hidden_size > 2:
+        gathered = combine(spread_sums, patches, hidden_size)
+    else:
+        received = lax.psum_scatter(spread_sums, "patch", scatter_dimension=0, tiled=True)
+        gathered = lax.all_gather(received, "hidden", axis=1, tiled=True)[None]
     mesh_out = mesh_finish(
         column,
         mesh_latent,
@@ -233,7 +412,7 @@
 
 def solution(mesh):
     return jax.shard_map(
-        functools.partial(shards, mesh.shape["hidden"]),
+        functools.partial(shards, mesh.shape["patch"], mesh.shape["hidden"]),
         mesh=mesh,
         in_specs=(
             P("patch", None),

time: 571 us -> 472 us (0.83)
  waiting for transfers between devices: 299 us -> 64.2 us
  Pallas kernels: 29.5 us -> 162 us
  other arithmetic: 94.5 us -> 85.5 us
  local copies, waits for them, and re-layouts: 109 us -> 117 us
    reduce_scatter x1 -> x0, waiting for transfers between devices: 179 us -> none  [shards(): lax.psum_scatter(spread_sums.astype(jnp.bfloat16), 'patch', scatter_dimen...]
    pallas_call x0 -> x1, Pallas kernels: none -> 133 us  [combine(): pl.pallas_call(functools.partial(combine_kernel, (outer_size, far_size, c...]
    all_gather x1, waiting for transfers between devices: 68 us -> 41.2 us  [shards(): table = lax.all_gather(receiver_part, 'patch', axis=0, tiled=True)]
    all_gather x1 -> x0, waiting for transfers between devices: 22.2 us -> none  [shards(): gathered = lax.all_gather(received, 'hidden', axis=1, tiled=True)]
    ppermute x9, waiting for transfers between devices: 29 us -> 15.1 us  [pieces(): lax.ppermute(x, 'hidden', [((j + k) % size, j) for j in range(size)])]
    all_gather x2, waiting for transfers between devices: 0.01 us -> 7.85 us  [shards(): gathered_hidden = lax.all_gather(edge_hidden, 'hidden', axis=1, tiled=True)]
    select_n x2 -> x0, other arithmetic: 7.51 us -> none  [the longest x1 7.5 us: shards(): sent = jnp.take(sender_part, sender_local, axis=0)]
  transfers between devices with their start and end apart: 14 -> 12, of which waited for: 8 -> 3; matrix products, arithmetic and copies ran while one was open for 26% -> 31% of each run, Pallas kernels for 1% -> 2%
where the time goes in v2:
time: 472 us; the launch traced here: 471 us
  Pallas kernels  162 us (34%)
  local copies, waits for them, and re-layouts  117 us (25%)
  other arithmetic  85.5 us (18%)
  waiting for transfers between devices  64.2 us (14%)
  matrix products  18.5 us (4%)
  between operations  14.8 us (3%)
  starting transfers between devices  8.91 us (2%)
    pallas_call x1, Pallas kernels, combine(): pl.pallas_call(functools.partial(combine_kernel, (outer_size, far_size, c...  133 us
    gather x4, local copies, waits for them, and re-layouts, rows_at(): return x.at[index].get(mode='promise_in_bounds')  106 us
    scatter-add x2, other arithmetic, shards(): spread_sums.at[target_rows[rows]].add(message, mode='promise_in_bounds')  65.4 us
    all_gather x1, waiting for transfers between devices, shards(): table = lax.all_gather(receiver_part, 'patch', axis=0, tiled=True)  41.2 us
    pallas_call x2, Pallas kernels, edge_finish(): pl.pallas_call(edge_kernel, grid_spec=pltpu.PrefetchScalarGridSpec(num_sc...  15.4 us
    ppermute x9, waiting for transfers between devices, pieces(): lax.ppermute(x, 'hidden', [((j + k) % size, j) for j in range(size)])  15.1 us
    pallas_call x1, Pallas kernels, mesh_finish(): pl.pallas_call(mesh_kernel, grid_spec=pltpu.PrefetchScalarGridSpec(num_sc...  13.8 us
    convert_element_type x1, other arithmetic, shards(): spread_sums = spread_sums.astype(jnp.bfloat16)  12 us
  transfers between devices with their start and end apart: 12, of which 3 were waited for; matrix products, arithmetic and copies ran while one was open for 31% of the time, Pallas kernels for 2%

profile of v2, /device:TPU:0, one launch (start us, length us, event | category | flops | bytes accessed | tf_op | source)
XLA Modules:
  0.0 471.0 jit_solution(9781080190224089991)
XLA Ops:
  7.2 0.0 copy-start
  7.2 0.0 copy-start.15
  7.2 0.0 copy-start.16
  7.2 0.0 copy-start.17
  7.2 0.0 copy-start.8
  7.2 0.0 all-gather.4.cloned.1.call-start
  7.3 5.2 %convolution_convert_fusion = bf16[5120,128]{1,0:T(8,128)(2,1)} fusion(bf16[5120,512]{1,0:T(8,128)(2,1)} %own_ref.1, bf16[512,128]{1,0:T(8,128)(2,1)} %param.31), kind=kOutput, calls=%fused_computation.8 | convolution fusion | flops 671744000 | bytes 6684672 | tf_op jit(solution)/shard_map/dot_general | solution.py:340
  12.5 0.0 all-gather.4.cloned.1.call-update
  12.5 0.0 all-gather.6.cloned.1.call-start
  12.6 0.5 collective-permute-start.8
  13.2 2.6 collective-permute-start.7
  15.7 1.4 collective-permute-start.6
  17.1 0.7 constant_dynamic-update-slice_fusion.5
  17.8 1.6 constant_dynamic-update-slice_fusion.4
  19.3 0.0 collective-permute-start.5
  19.3 0.7 constant_dynamic-update-slice_fusion.1
  20.1 1.6 constant_dynamic-update-slice_fusion
  21.6 1.7 collective-permute-start
  23.4 0.0 copy-done
  23.4 0.0 copy-start.14
  23.4 0.0 copy-start.3
  23.4 3.1 fusion.30
  26.6 0.0 copy-start.4
  26.6 45.5 %gather_fusion = s32[8192]{0:T(1024)S(1)} fusion(s32[40960]{0:T(1024)S(1)} %copy-done.3, s32[8192]{0:T(1024)S(1)} %fusion.21), kind=kCustom, calls=%fused_computation | custom fusion | bytes 98304 | tf_op jit(solution)/shard_map/gather | solution.py:298
  72.1 27.7 %gather_fusion.1 = f32[8192,128]{1,0:T(8,128)} fusion(f32[3072,128]{1,0:T(8,128)S(1)} %copy-done.4, s32[8192]{0:T(1024)S(1)} %fusion.22), kind=kCustom, calls=%fused_computation.1 | custom fusion | bytes 8421376 | tf_op jit(solution)/shard_map/gather | solution.py:298
  99.9 0.0 collective-permute-done.8
  99.9 0.4 collective-permute-start.4
  100.2 0.0 collective-permute-done.7
  100.2 0.0 collective-permute-start.3
  100.2 0.0 collective-permute-done.6
  100.2 1.8 collective-permute-start.1
  102.0 0.0 collective-permute-done
  102.0 0.2 collective-permute-start.2
  102.3 1.0 fusion.28
  103.2 15.1 %collective-permute-done.1 = bf16[256,512]{1,0:T(8,128)(2,1)S(1)} collective-permute-done((bf16[256,512]{1,0:T(8,128)(2,1)}, bf16[256,512]{1,0:T(8,128)(2,1)S(1)}, u32[]{:S(2)}, u32[]{:S(2)}) %collective-permute-start.1) | collective-permute-done | bytes 262176 | tf_op jit(solution)/shard_map/ppermute | solution.py:293
  118.4 0.0 collective-permute-done.2
  118.4 0.0 copy-start.11
  118.4 0.9 slice_dynamic-update-slice_fusion.5
  119.4 0.0 collective-permute-done.5
  119.4 1.0 fusion.25
  120.5 0.0 collective-permute-done.4
  120.5 0.0 collective-permute-done.3
  120.6 1.1 pad_maximum_fusion.1
  121.7 3.0 fusion.16
  124.7 41.2 %all-gather.4.cloned.1.call-done = bf16[40960,128]{1,0:T(8,128)(2,1)} async-done(((bf16[5120,128]{1,0:T(8,128)(2,1)}), bf16[40960,128]{1,0:T(8,128)(2,1)}) %all-gather.4.cloned.1.call-update) | async-done | bytes 10485776 | tf_op jit(solution)/shard_map/all_gather | solution.py:343
  165.9 16.4 %gather_fusion.2 = bf16[4096,128]{1,0:T(8,128)(2,1)S(1)} fusion(bf16[40960,128]{1,0:T(8,128)(2,1)} %all-gather.4.cloned.1.call-done, s32[4096]{0:T(1024)S(1)} %get-tuple-element.37), kind=kCustom, calls=%fused_computation.2 | custom fusion | bytes 2113536 | tf_op jit(solution)/shard_map/gather | solution.py:298
  182.4 5.1 %multiply_convert_fusion.1 = bf16[4096,128]{1,0:T(8,128)(2,1)} fusion(f32[8192,128]{1,0:T(8,128)} %gather_fusion.1, bf16[512,128]{1,0:T(8,128)(2,1)S(1)} %copy-done.18, bf16[8192,512]{1,0:T(8,128)(2,1)} %latent_ref.4, bf16[4096,128]{1,0:T(8,128)(2,1)S(1)} %gather_fusion.2, f32[128]{0:T(128)S(1)} %copy-done.19), kind=kOutput, calls=%fused_computation.21 | convolution fusion | flops 541589504 | bytes 8520192 | tf_op jit(solution)/shard_map/dot_general | solution.py:370
  187.5 0.0 all-gather.6.cloned.1.call-update
  187.5 0.2 all-gather.8.cloned.1.call-start
  187.7 16.4 %gather_fusion.3 = bf16[4096,128]{1,0:T(8,128)(2,1)S(1)} fusion(bf16[40960,128]{1,0:T(8,128)(2,1)} %all-gather.4.cloned.1.call-done, s32[4096]{0:T(1024)S(1)} %get-tuple-element.36), kind=kCustom, calls=%fused_computation.3 | custom fusion | bytes 2113536 | tf_op jit(solution)/shard_map/gather | solution.py:298
  204.1 5.1 %multiply_convert_fusion = bf16[4096,128]{1,0:T(8,128)(2,1)} fusion(f32[8192,128]{1,0:T(8,128)} %gather_fusion.1, bf16[512,128]{1,0:T(8,128)(2,1)S(1)} %copy-done.18, bf16[8192,512]{1,0:T(8,128)(2,1)} %latent_ref.4, bf16[4096,128]{1,0:T(8,128)(2,1)S(1)} %gather_fusion.3, f32[128]{0:T(128)S(1)} %copy-done.19), kind=kOutput, calls=%fused_computation.20 | convolution fusion | flops 541589504 | bytes 8520192 | tf_op jit(solution)/shard_map/dot_general | solution.py:370
  209.3 0.0 all-gather.8.cloned.1.call-update
  209.9 2.4 fusion.8.live_ref
  212.4 0.6 fusion.29
  213.0 7.9 %all-gather.6.cloned.1.call-done.hidden_ref = bf16[4096,512]{1,0:T(8,128)(2,1)} async-done(((bf16[4096,128]{1,0:T(8,128)(2,1)}), bf16[4096,512]{1,0:T(8,128)(2,1)}) %all-gather.6.cloned.1.call-update) | async-done | bytes 4194320 | tf_op jit(solution)/shard_map/all_gather | solution.py:376
  220.8 7.7 %edge_finish.2 = (f32[4096,128]{1,0:T(8,128)}, bf16[4096,128]{1,0:T(8,128)(2,1)}) custom-call(s32[1]{0:T(128)} %bitcast.column, bf16[4096,512]{1,0:T(8,128)(2,1)} %all-gather.6.cloned.1.call-done.hidden_ref, bf16[8192,512]{1,0:T(8,128)(2,1)} %latent_ref.4, f32[8192,1]{1,0:T(8,128)} %fusion.8.live_ref, bf16[512,512]{1,0:T(8,128)(2,1)} %get-tuple-element.13.w_ref, ...), custom_call_target="tpu_custom_call" | custom-call | flops 2147483648 | bytes 8388608 | tf_op jit(solution)/shard_map/edge_finish/pallas_call | solution.py:50
  228.5 31.1 %scatter_custom_fusion = f32[40960,128]{1,0:T(8,128)} fusion(s32[4096]{0:T(1024)S(1)} %get-tuple-element.39, f32[4096,128]{1,0:T(8,128)} %get-tuple-element.15, f32[]{:T(128)} %constant.13.clone.1), kind=kCustom, calls=%fused_computation.6 | custom fusion | flops 524288 | bytes 20972032 | tf_op jit(solution)/shard_map/scatter-add | solution.py:389
  259.6 7.7 %edge_finish.3 = (f32[4096,128]{1,0:T(8,128)}, bf16[4096,128]{1,0:T(8,128)(2,1)}) custom-call(s32[1]{0:T(128)} %bitcast.column, bf16[4096,512]{1,0:T(8,128)(2,1)} %all-gather.8.cloned.1.call-done.hidden_ref, bf16[8192,512]{1,0:T(8,128)(2,1)} %latent_ref.4, f32[8192,1]{1,0:T(8,128)} %fusion.8.live_ref, bf16[512,512]{1,0:T(8,128)(2,1)} %get-tuple-element.13.w_ref, ...), custom_call_target="tpu_custom_call" | custom-call | flops 2147483648 | bytes 8388608 | tf_op jit(solution)/shard_map/edge_finish/pallas_call | solution.py:50
  267.3 34.4 %scatter_fusion = f32[40960,128]{1,0:T(8,128)} fusion(f32[40960,128]{1,0:T(8,128)} %scatter_custom_fusion, s32[4096]{0:T(1024)S(1)} %get-tuple-element.38, f32[4096,128]{1,0:T(8,128)} %get-tuple-element.16), kind=kCustom, calls=%fused_computation.5 | custom fusion | flops 524288 | bytes 6307840 | tf_op jit(solution)/shard_map/scatter-add | solution.py:389
  301.7 12.0 %convert_element_type.34 = bf16[40960,128]{1,0:T(8,128)(2,1)} convert(f32[40960,128]{1,0:T(8,128)} %scatter_fusion) | non-fusion elementwise | flops 5242880 | bytes 31457280 | tf_op jit(solution)/shard_map/convert_element_type | solution.py:392
  313.7 133.2 %combine.1.summed_ref = bf16[4,5120,128]{2,1,0:T(8,128)(2,1)S(1)} custom-call(bf16[4,2,5120,128]{3,2,1,0:T(8,128)(2,1)} %bitcast.17), custom_call_target="tpu_custom_call" | custom-call | tf_op jit(solution)/shard_map/combine/pallas_call | solution.py:261
  446.9 2.3 copy-done.2
  449.2 1.5 pad_maximum_fusion
  450.7 13.8 %mesh_finish.1 = bf16[5120,128]{1,0:T(8,128)(2,1)} custom-call(s32[1]{0:T(128)} %bitcast.column, bf16[5120,512]{1,0:T(8,128)(2,1)} %own_ref.1, bf16[5120,512]{1,0:T(8,128)(2,1)} %own_ref.1, bf16[4,5120,128]{2,1,0:T(8,128)(2,1)} %copy-done.2, bf16[512,512]{1,0:T(8,128)(2,1)} %get-tuple-element.17.w_in_ref, bf16[512,512]{1,0:T(8,128)(2,1)} %get-tuple-element.18.w_msg_ref, ...), custom_call_target="tpu_custom_call" | custom-call | flops 8053063680 | bytes 13107200 | tf_op jit(solution)/shard_map/mesh_finish/pallas_call | solution.py:96
  (43 shorter events, 0.3 us)
Async XLA Ops:
  7.2 16.2 %copy-start = (bf16[3072,512]{1,0:T(8,128)(2,1)S(1)}, bf16[3072,512]{1,0:T(8,128)(2,1)}, u32[]{:S(2)}) copy-start(bf16[3072,512]{1,0:T(8,128)(2,1)} %param.22) | copy-start | bytes 9437188
  7.2 5.4 %copy-start.15 = (f32[128]{0:T(128)S(1)}, f32[128]{0:T(128)}, u32[]{:S(2)}) copy-start(f32[128]{0:T(128)} %param.41) | copy-start | bytes 1540
  7.2 5.4 %copy-start.16 = (f32[128]{0:T(128)S(1)}, f32[128]{0:T(128)}, u32[]{:S(2)}) copy-start(f32[128]{0:T(128)} %param.39) | copy-start | bytes 1540
  7.2 5.4 %copy-start.17 = (f32[128]{0:T(128)S(1)}, f32[128]{0:T(128)}, u32[]{:S(2)}) copy-start(f32[128]{0:T(128)} %param.34) | copy-start | bytes 1540
  7.2 9.9 %copy-start.8 = (bf16[512,128]{1,0:T(8,128)(2,1)S(1)}, bf16[512,128]{1,0:T(8,128)(2,1)}, u32[]{:S(2)}) copy-start(bf16[512,128]{1,0:T(8,128)(2,1)} %param.37) | copy-start | bytes 393220
  7.2 12.1 %copy-start.7 = (bf16[128,512]{1,0:T(8,128)(2,1)S(1)}, bf16[128,512]{1,0:T(8,128)(2,1)}, u32[]{:S(2)}) copy-start(bf16[128,512]{1,0:T(8,128)(2,1)} %param.33) | copy-start | bytes 393220
  7.2 16.1 %copy-start.13 = (s32[8192]{0:T(1024)S(1)}, s32[8192]{0:T(1024)}, u32[]{:S(2)}) copy-start(s32[8192]{0:T(1024)} %param.26) | copy-start | bytes 98308
  7.2 158.7 %all-gather.4.cloned.1.call-start = ((), (), s32[]{:S(2)}) async-start(), calls=%async_computation | async-start | bytes 11796480 | tf_op jit(solution)/shard_map/all_gather | solution.py:343
  12.5 208.3 %all-gather.6.cloned.1.call-start = ((), (), s32[]{:S(2)}) async-start(), calls=%async_computation.1 | async-start | bytes 5242880 | tf_op jit(solution)/shard_map/all_gather | solution.py:376
  12.6 87.2 %collective-permute-start.8 = (f32[3,128]{1,0:T(4,128)S(1)}, f32[3,128]{1,0:T(4,128)S(1)}, u32[]{:S(2)}, u32[]{:S(2)}) collective-permute-start(f32[3,128]{1,0:T(4,128)S(1)} %pad_maximum_fusion.4), channel_id=1, source_target_pairs={{3,0},{0,1},{1,2},{2,3},{7,4},{4,5},{5,6},{6,7},{11,8},{8,9},{9,10... | collective-permute-start | bytes 4616 | tf_op jit(solution)/shard_map/ppermute | solution.py:293
  13.2 87.0 %collective-permute-start.7 = (f32[3,128]{1,0:T(4,128)S(1)}, f32[3,128]{1,0:T(4,128)S(1)}, u32[]{:S(2)}, u32[]{:S(2)}) collective-permute-start(f32[3,128]{1,0:T(4,128)S(1)} %pad_maximum_fusion.4), channel_id=1, source_target_pairs={{2,0},{3,1},{0,2},{1,3},{6,4},{7,5},{4,6},{5,7},{10,8},{11,9},{8,1... | collective-permute-start | bytes 4616 | tf_op jit(solution)/shard_map/ppermute | solution.py:293
  15.7 84.5 %collective-permute-start.6 = (f32[3,128]{1,0:T(4,128)S(1)}, f32[3,128]{1,0:T(4,128)S(1)}, u32[]{:S(2)}, u32[]{:S(2)}) collective-permute-start(f32[3,128]{1,0:T(4,128)S(1)} %pad_maximum_fusion.4), channel_id=1, source_target_pairs={{1,0},{2,1},{3,2},{0,3},{5,4},{6,5},{7,6},{4,7},{9,8},{10,9},{11,1... | collective-permute-start | bytes 4616 | tf_op jit(solution)/shard_map/ppermute | solution.py:293
  19.3 100.1 %collective-permute-start.5 = (bf16[1024,128]{1,0:T(8,128)(2,1)}, bf16[1024,128]{1,0:T(8,128)(2,1)}, u32[]{:S(2)}, u32[]{:S(2)}) collective-permute-start(bf16[1024,128]{1,0:T(8,128)(2,1)} %constant_dynamic-update-slice_fusion.4), channel_id=1, source_target_pairs={{3,0},{0,1},{1,2},{2,3},{7,4},{4,5},{5,6},{6,7},{11,8},{8,9},{9,10... | collective-permute-start | bytes 786440 | tf_op jit(solution)/shard_map/ppermute | solution.py:293
  21.6 80.4 %collective-permute-start = (bf16[256,512]{1,0:T(8,128)(2,1)}, bf16[256,512]{1,0:T(8,128)(2,1)}, u32[]{:S(2)}, u32[]{:S(2)}) collective-permute-start(bf16[256,512]{1,0:T(8,128)(2,1)} %constant_dynamic-update-slice_fusion), channel_id=1, source_target_pairs={{1,0},{2,1},{3,2},{0,3},{5,4},{6,5},{7,6},{4,7},{9,8},{10,9},{11,1... | collective-permute-start | bytes 786440 | tf_op jit(solution)/shard_map/ppermute | solution.py:293
  23.4 3.1 copy-start.14
  23.4 3.1 copy-start.3
  26.6 45.6 %copy-start.4 = (f32[3072,128]{1,0:T(8,128)S(1)}, f32[3072,128]{1,0:T(8,128)}, u32[]{:S(2)}) copy-start(f32[3072,128]{1,0:T(8,128)} %fusion.30) | copy-start | bytes 4718596
  72.1 30.1 %copy-start.12 = (bf16[1024,512]{1,0:T(8,128)(2,1)S(1)}, bf16[1024,512]{1,0:T(8,128)(2,1)}, u32[]{:S(2)}) copy-start(bf16[1024,512]{1,0:T(8,128)(2,1)} %get-tuple-element.35) | copy-start | bytes 3145732
  99.9 20.7 %copy-start.9 = (bf16[512,128]{1,0:T(8,128)(2,1)S(1)}, bf16[512,128]{1,0:T(8,128)(2,1)}, u32[]{:S(2)}) copy-start(bf16[512,128]{1,0:T(8,128)(2,1)} %param.37) | copy-start | bytes 393220
  99.9 20.7 %copy-start.10 = (bf16[512,128]{1,0:T(8,128)(2,1)S(1)}, bf16[512,128]{1,0:T(8,128)(2,1)}, u32[]{:S(2)}) copy-start(bf16[512,128]{1,0:T(8,128)(2,1)} %param.38) | copy-start | bytes 393220
  99.9 20.6 %collective-permute-start.4 = (bf16[1024,128]{1,0:T(8,128)(2,1)}, bf16[1024,128]{1,0:T(8,128)(2,1)S(1)}, u32[]{:S(2)}, u32[]{:S(2)}) collective-permute-start(bf16[1024,128]{1,0:T(8,128)(2,1)} %constant_dynamic-update-slice_fusion.4), channel_id=1, source_target_pairs={{2,0},{3,1},{0,2},{1,3},{6,4},{7,5},{4,6},{5,7},{10,8},{11,9},{8,1... | collective-permute-start | bytes 786440 | tf_op jit(solution)/shard_map/ppermute | solution.py:293
  100.2 20.3 %collective-permute-start.3 = (bf16[1024,128]{1,0:T(8,128)(2,1)}, bf16[1024,128]{1,0:T(8,128)(2,1)S(1)}, u32[]{:S(2)}, u32[]{:S(2)}) collective-permute-start(bf16[1024,128]{1,0:T(8,128)(2,1)} %constant_dynamic-update-slice_fusion.4), channel_id=1, source_target_pairs={{1,0},{2,1},{3,2},{0,3},{5,4},{6,5},{7,6},{4,7},{9,8},{10,9},{11,1... | collective-permute-start | bytes 786440 | tf_op jit(solution)/shard_map/ppermute | solution.py:293
  100.2 18.1 %collective-permute-start.1 = (bf16[256,512]{1,0:T(8,128)(2,1)}, bf16[256,512]{1,0:T(8,128)(2,1)S(1)}, u32[]{:S(2)}, u32[]{:S(2)}) collective-permute-start(bf16[256,512]{1,0:T(8,128)(2,1)} %constant_dynamic-update-slice_fusion), channel_id=1, source_target_pairs={{2,0},{3,1},{0,2},{1,3},{6,4},{7,5},{4,6},{5,7},{10,8},{11,9},{8,1... | collective-permute-start | bytes 786440 | tf_op jit(solution)/shard_map/ppermute | solution.py:293
  102.0 16.3 %collective-permute-start.2 = (bf16[256,512]{1,0:T(8,128)(2,1)}, bf16[256,512]{1,0:T(8,128)(2,1)S(1)}, u32[]{:S(2)}, u32[]{:S(2)}) collective-permute-start(bf16[256,512]{1,0:T(8,128)(2,1)} %constant_dynamic-update-slice_fusion), channel_id=1, source_target_pairs={{3,0},{0,1},{1,2},{2,3},{7,4},{4,5},{5,6},{6,7},{11,8},{8,9},{9,10... | collective-permute-start | bytes 786440 | tf_op jit(solution)/shard_map/ppermute | solution.py:293
  118.4 3.3 copy-start.11
  165.9 16.4 %copy-start.18 = (bf16[512,128]{1,0:T(8,128)(2,1)S(1)}, bf16[512,128]{1,0:T(8,128)(2,1)}, u32[]{:S(2)}) copy-start(bf16[512,128]{1,0:T(8,128)(2,1)} %param.29) | copy-start | bytes 393220
  165.9 16.4 %copy-start.19 = (f32[128]{0:T(128)S(1)}, f32[128]{0:T(128)}, u32[]{:S(2)}) copy-start(f32[128]{0:T(128)} %param.32) | copy-start | bytes 1540
  187.5 72.1 %all-gather.8.cloned.1.call-start = ((), (), s32[]{:S(2)}) async-start(), calls=%async_computation.2 | async-start | bytes 5242880 | tf_op jit(solution)/shard_map/all_gather | solution.py:376
  313.7 135.5 %copy-start.5 = (bf16[4096,128]{1,0:T(8,128)(2,1)S(1)}, bf16[4096,128]{1,0:T(8,128)(2,1)}, u32[]{:S(2)}) copy-start(bf16[4096,128]{1,0:T(8,128)(2,1)} %get-tuple-element.20) | copy-start | bytes 3145732
  313.7 135.5 %copy-start.6 = (bf16[4096,128]{1,0:T(8,128)(2,1)S(1)}, bf16[4096,128]{1,0:T(8,128)(2,1)}, u32[]{:S(2)}) copy-start(bf16[4096,128]{1,0:T(8,128)(2,1)} %get-tuple-element.21) | copy-start | bytes 3145732
  446.9 2.3 copy-start.2
  450.7 13.8 %copy-start.1 = (bf16[3072,512]{1,0:T(8,128)(2,1)S(1)}, bf16[3072,512]{1,0:T(8,128)(2,1)}, u32[]{:S(2)}) copy-start(bf16[3072,512]{1,0:T(8,128)(2,1)} %param.22) | copy-start | bytes 9437188
Sparse Core Ops, SparseCore 0:
  12.7 153.2 all-gather.3
  187.6 33.1 all-gather.5
  222.4 34.9 all-gather.7

commit v3 on v2

--- a/solution.py
+++ b/solution.py
@@ -34,28 +34,30 @@
     return cut, pl.BlockSpec((block, own), lambda i, c: (i + first, 0))
 
 
-def edge_kernel(column, hidden_ref, latent_ref, live_ref, w_ref, bias_ref, gain_ref, shift_ref, message_ref, out_ref):
+def edge_kernel(first_row, scalars, hidden_ref, latent_ref, w_ref, bias_ref, gain_ref, shift_ref, message_ref, out_ref):
     total = jnp.dot(hidden_ref[...], w_ref[...], preferred_element_type=jnp.float32) + bias_ref[...]
-    message = norm_own(total, gain_ref[...], shift_ref[...]) * live_ref[...]
+    start = first_row + pl.program_id(0) * total.shape[0]
+    slot = start + lax.broadcasted_iota(jnp.int32, message_ref.shape, 0)
+    message = norm_own(total, gain_ref[...], shift_ref[...])
+    message = jnp.where(slot < scalars[1], message, 0.0)
     message_ref[...] = message
     out_ref[...] = (latent_ref[...].astype(jnp.float32) + message).astype(out_ref.dtype)
 
 
-def edge_finish(column, hidden, latent, first_row, live, w_out, bias, gain, shift):
+def edge_finish(column, hidden, latent, first_row, w_out, bias, gain, shift):
     rows, full = hidden.shape
     own = gain.shape[1]
     block = row_block(rows, 1024)
     first = first_row // block
     latent, latent_spec = own_columns(column, latent, own, block, first)
     return pl.pallas_call(
-        edge_kernel,
+        functools.partial(edge_kernel, first_row),
         grid_spec=pltpu.PrefetchScalarGridSpec(
             num_scalar_prefetch=1,
             grid=(rows // block,),
             in_specs=[
                 pl.BlockSpec((block, full), lambda i, c: (i, 0)),
                 latent_spec,
-                pl.BlockSpec((block, 1), lambda i, c: (i + first, 0)),
                 pl.BlockSpec((full, full), lambda i, c: (0, 0)),
                 pl.BlockSpec((1, full), lambda i, c: (0, 0)),
                 pl.BlockSpec((1, own), lambda i, c: (0, 0)),
@@ -74,7 +76,7 @@
             flops=2 * rows * full * full, bytes_accessed=2 * rows * full + 8 * rows * own, transcendentals=0
         ),
         name="edge_finish",
-    )(column, hidden, latent, live, w_out, bias, gain, shift)
+    )(column, hidden, latent, w_out, bias, gain, shift)
 
 
 def mesh_kernel(column, latent_ref, own_ref, summed_ref, w_in_ref, w_msg_ref, bias_in_ref, w_out_ref, bias_ref, gain_ref, shift_ref, out_ref):
@@ -120,7 +122,7 @@
     )(column, latent, own_latent, summed, w_in, w_msg, bias_in, w_out, bias, gain, shift)
 
 
-def combine_kernel(sizes, part_ref, out_ref, own, paired, crossed, gathered, own_sem, pair_send, pair_recv, cross_send, cross_recv, side_send, side_recv, far_send, far_recv, relay_send, relay_recv, out_sem):
+def combine_kernel(sizes, part_ref, out_ref, stage, leaving, own, paired, crossed, gathered, own_sem, pair_send, pair_recv, cross_send, cross_recv, side_send, side_recv, far_send, far_recv, relay_send, relay_recv, out_sem):
     outer_size, far_size, chunks, rows = sizes
     patch, rank = lax.axis_index("patch"), lax.axis_index("hidden")
     outer, inner = patch // 2, patch % 2
@@ -155,13 +157,31 @@
         return pl.ds(c * rows, rows)
 
     loads, pairs, crosses, sides, fars, relays, outs = [], {}, {}, {}, {}, {}, []
+    tile = row_block(rows, 128)
+
+    def load(c):
+        copy = pltpu.make_async_copy(part_ref.at[:, :, span(c)], stage.at[c % 2], own_sem.at[c])
+        copy.start()
+        loads.append(copy)
+
+    load(0)
+    load(1)
     for c in range(chunks):
-        load = pltpu.make_async_copy(part_ref.at[:, inner, span(c)], own.at[c], own_sem.at[c])
-        load.start()
-        loads.append(load)
+        loads[c].wait()
+
+        def narrow(i, carry):
+            at = pl.ds(pl.multiple_of(i * tile, tile), tile)
+            for block in range(outer_size):
+                own[c, block, at] = stage[c % 2, block, inner, at].astype(jnp.bfloat16)
+                leaving[c, block, at] = stage[c % 2, block, 1 - inner, at].astype(jnp.bfloat16)
+            return carry
+
+        lax.fori_loop(0, rows // tile, narrow, 0)
+        if c + 2 < chunks:
+            load(c + 2)
         for k in range(outer_size):
             pairs[c, k] = send(
-                part_ref.at[blocks[k], 1 - inner, span(c)],
+                leaving.at[c, blocks[k]],
                 paired.at[c, k],
                 pair_send.at[c, k],
                 pair_recv.at[c, k],
@@ -169,10 +189,7 @@
                 pair_peer,
             )
 
-    tile = row_block(rows, 128)
-
     def reduce_pair(c):
-        loads[c].wait()
         for k in range(outer_size - 1):
             pairs[c, k].wait_recv()
 
@@ -253,7 +270,7 @@
     total_rows, width = parts.shape
     rows = total_rows // patches
     outer_size, far_size = patches // 2, ranks // 2
-    chunks = 5 if rows % 80 == 0 else 4
+    chunks = 10 if rows % 160 == 0 else 4
     size = rows // chunks
     dma = pltpu.SemaphoreType.DMA
     cross = (chunks, outer_size - 1)
@@ -264,6 +281,8 @@
         out_specs=pl.BlockSpec(memory_space=pl.ANY),
         out_shape=jax.ShapeDtypeStruct((ranks, rows, width), jnp.bfloat16),
         scratch_shapes=[
+            pltpu.VMEM((2, outer_size, 2, size, width), jnp.float32),
+            pltpu.VMEM((chunks, outer_size, size, width), jnp.bfloat16),
             pltpu.VMEM((chunks, outer_size, size, width), jnp.bfloat16),
             pltpu.VMEM((chunks, outer_size, size, width), jnp.bfloat16),
             pltpu.VMEM(cross + (size, width), jnp.bfloat16),
@@ -335,7 +354,7 @@
     width = w_edge.shape[1]
     full = w_edge.shape[0]
     mesh_total = mesh_slot.shape[0]
-    column = jnp.reshape(column_index, (1,)).astype(jnp.int32)
+    column = jnp.stack([column_index.astype(jnp.int32), edge_counts[0]])
 
     receiver_part = jnp.dot(mesh_latent, w_receiver, preferred_element_type=jnp.float32).astype(
         jnp.bfloat16
@@ -357,7 +376,6 @@
     target_rows, weights = lax.optimization_barrier((target_rows, weights))
     edge_w_out, mesh_w_out, mesh_w_in, mesh_w_msg, biases = weights
     sender_local = senders - patch_index * own_grid
-    live = (jnp.arange(own_edges, dtype=jnp.int32) < edge_counts[0]).astype(jnp.float32)[:, None]
     sender_part = jnp.dot(grid_latent, w_sender, preferred_element_type=jnp.float32)
     sent = rows_at(sender_part, sender_local)
 
@@ -379,7 +397,6 @@
             gathered_hidden,
             edge_latent,
             at,
-            live,
             edge_w_out,
             biases[:1],
             edge_gain[None],
@@ -389,11 +406,12 @@
         spread_sums = spread_sums.at[target_rows[rows]].add(message, mode="promise_in_bounds")
     edge_out = jnp.concatenate(edge_outs, 0)
 
-    spread_sums = spread_sums.astype(jnp.bfloat16)
     if width % 128 == 0 and patches % 2 == 0 and patches > 2 and hidden_size % 2 == 0 and hidden_size > 2:
         gathered = combine(spread_sums, patches, hidden_size)
     else:
-        received = lax.psum_scatter(spread_sums, "patch", scatter_dimension=0, tiled=True)
+        received = lax.psum_scatter(
+            spread_sums.astype(jnp.bfloat16), "patch", scatter_dimension=0, tiled=True
+        )
         gathered = lax.all_gather(received, "hidden", axis=1, tiled=True)[None]
     mesh_out = mesh_finish(
         column,

time: 472 us -> 460 us (0.975)
  other arithmetic: 85.5 us -> 71.7 us
    convert_element_type x2 -> x0, other arithmetic: 14.4 us -> none  [the longest x1 12 us: shards(): spread_sums = spread_sums.astype(jnp.bfloat16)]
where the time goes in v3:
time: 460 us; the launch traced here: 459 us
  Pallas kernels  162 us (35%)
  local copies, waits for them, and re-layouts  117 us (25%)
  other arithmetic  71.7 us (16%)
  waiting for transfers between devices  66.1 us (14%)
  matrix products  18.5 us (4%)
  between operations  14.8 us (3%)
  starting transfers between devices  8.84 us (2%)
    pallas_call x1, Pallas kernels, combine(): pl.pallas_call(functools.partial(combine_kernel, (outer_size, far_size, c...  132 us
    gather x4, local copies, waits for them, and re-layouts, rows_at(): return x.at[index].get(mode='promise_in_bounds')  106 us
    scatter-add x2, other arithmetic, shards(): spread_sums.at[target_rows[rows]].add(message, mode='promise_in_bounds')  65.5 us
    all_gather x1, waiting for transfers between devices, shards(): table = lax.all_gather(receiver_part, 'patch', axis=0, tiled=True)  41.3 us
    pallas_call x2, Pallas kernels, edge_finish(): pl.pallas_call(functools.partial(edge_kernel, first_row), grid_spec=pltpu...  15.9 us
    ppermute x9, waiting for transfers between devices, pieces(): lax.ppermute(x, 'hidden', [((j + k) % size, j) for j in range(size)])  15.1 us
    pallas_call x1, Pallas kernels, mesh_finish(): pl.pallas_call(mesh_kernel, grid_spec=pltpu.PrefetchScalarGridSpec(num_sc...  14.6 us
    dot_general x2, matrix products, shards(): jnp.dot(edge_latent[rows], w_edge, preferred_element_type=jnp.float32)  10.2 us
  transfers between devices with their start and end apart: 12, of which 3 were waited for; matrix products, arithmetic and copies ran while one was open for 31% of the time, Pallas kernels for 2%

profile of v3, /device:TPU:0, one launch (start us, length us, event | category | flops | bytes accessed | tf_op | source)
XLA Modules:
  0.0 459.0 jit_solution(11043513995759359585)
XLA Ops:
  7.2 0.0 copy-start
  7.2 0.0 copy-start.8
  7.2 0.0 all-gather.4.cloned.1.call-start
  7.3 5.2 %convolution_convert_fusion = bf16[5120,128]{1,0:T(8,128)(2,1)} fusion(bf16[5120,512]{1,0:T(8,128)(2,1)} %own_ref.1, bf16[512,128]{1,0:T(8,128)(2,1)} %param.31), kind=kOutput, calls=%fused_computation.8 | convolution fusion | flops 671744000 | bytes 6684672 | tf_op jit(solution)/shard_map/dot_general | solution.py:359
  12.5 0.0 all-gather.4.cloned.1.call-update
  12.5 0.0 all-gather.6.cloned.1.call-start
  12.6 0.6 collective-permute-start.8
  13.2 2.5 collective-permute-start.7
  15.7 1.4 collective-permute-start.6
  17.1 0.0 copy-done.8
  17.1 0.7 constant_dynamic-update-slice_fusion.5
  17.8 1.6 constant_dynamic-update-slice_fusion.4
  19.3 0.0 collective-permute-start.5
  19.3 0.0 copy-done.7
  19.3 0.7 constant_dynamic-update-slice_fusion.1
  20.0 1.6 constant_dynamic-update-slice_fusion
  21.6 1.7 collective-permute-start
  23.4 0.0 copy-start.14
  23.4 0.0 copy-start.3
  23.4 3.1 fusion.29
  26.5 0.0 copy-start.4
  26.5 45.5 %gather_fusion = s32[8192]{0:T(1024)S(1)} fusion(s32[40960]{0:T(1024)S(1)} %copy-done.3, s32[8192]{0:T(1024)S(1)} %fusion.20), kind=kCustom, calls=%fused_computation | custom fusion | bytes 98304 | tf_op jit(solution)/shard_map/gather | solution.py:317
  72.1 27.7 %gather_fusion.1 = f32[8192,128]{1,0:T(8,128)} fusion(f32[3072,128]{1,0:T(8,128)S(1)} %copy-done.4, s32[8192]{0:T(1024)S(1)} %fusion.21), kind=kCustom, calls=%fused_computation.1 | custom fusion | bytes 8421376 | tf_op jit(solution)/shard_map/gather | solution.py:317
  99.8 0.0 collective-permute-done.8
  99.8 0.3 collective-permute-start.4
  100.1 0.0 collective-permute-done.7
  100.1 0.0 collective-permute-start.3
  100.1 0.0 collective-permute-done.6
  100.1 1.8 collective-permute-start.1
  101.9 0.0 collective-permute-done
  102.0 0.2 collective-permute-start.2
  102.2 1.0 fusion.27
  103.2 15.1 %collective-permute-done.1 = bf16[256,512]{1,0:T(8,128)(2,1)S(1)} collective-permute-done((bf16[256,512]{1,0:T(8,128)(2,1)}, bf16[256,512]{1,0:T(8,128)(2,1)S(1)}, u32[]{:S(2)}, u32[]{:S(2)}) %collective-permute-start.1) | collective-permute-done | bytes 262176 | tf_op jit(solution)/shard_map/ppermute | solution.py:312
  118.3 0.0 collective-permute-done.2
  118.3 0.0 copy-start.9
  118.3 0.0 copy-start.10
  118.4 1.0 slice_dynamic-update-slice_fusion.5
  119.4 0.0 collective-permute-done.5
  119.4 1.0 fusion.24
  120.4 0.0 copy-start.11
  120.4 0.0 collective-permute-done.4
  120.5 0.0 collective-permute-done.3
  120.5 1.1 pad_maximum_fusion.1
  121.7 3.0 fusion.15
  124.6 41.3 %all-gather.4.cloned.1.call-done = bf16[40960,128]{1,0:T(8,128)(2,1)} async-done(((bf16[5120,128]{1,0:T(8,128)(2,1)}), bf16[40960,128]{1,0:T(8,128)(2,1)}) %all-gather.4.cloned.1.call-update) | async-done | bytes 10485776 | tf_op jit(solution)/shard_map/all_gather | solution.py:362
  165.9 16.4 %gather_fusion.2 = bf16[4096,128]{1,0:T(8,128)(2,1)S(1)} fusion(bf16[40960,128]{1,0:T(8,128)(2,1)} %all-gather.4.cloned.1.call-done, s32[4096]{0:T(1024)S(1)} %get-tuple-element.37), kind=kCustom, calls=%fused_computation.2 | custom fusion | bytes 2113536 | tf_op jit(solution)/shard_map/gather | solution.py:317
  182.3 5.1 %multiply_convert_fusion.1 = bf16[4096,128]{1,0:T(8,128)(2,1)} fusion(f32[8192,128]{1,0:T(8,128)} %gather_fusion.1, bf16[512,128]{1,0:T(8,128)(2,1)S(1)} %copy-done.18, bf16[8192,512]{1,0:T(8,128)(2,1)} %latent_ref.4, bf16[4096,128]{1,0:T(8,128)(2,1)S(1)} %gather_fusion.2, f32[128]{0:T(128)S(1)} %copy-done.19), kind=kOutput, calls=%fused_computation.19 | convolution fusion | flops 541589504 | bytes 8520192 | tf_op jit(solution)/shard_map/dot_general | solution.py:388
  187.5 0.0 all-gather.6.cloned.1.call-update
  187.5 0.2 all-gather.8.cloned.1.call-start
  187.7 16.4 %gather_fusion.3 = bf16[4096,128]{1,0:T(8,128)(2,1)S(1)} fusion(bf16[40960,128]{1,0:T(8,128)(2,1)} %all-gather.4.cloned.1.call-done, s32[4096]{0:T(1024)S(1)} %get-tuple-element.36), kind=kCustom, calls=%fused_computation.3 | custom fusion | bytes 2113536 | tf_op jit(solution)/shard_map/gather | solution.py:317
  204.1 5.1 %multiply_convert_fusion = bf16[4096,128]{1,0:T(8,128)(2,1)} fusion(f32[8192,128]{1,0:T(8,128)} %gather_fusion.1, bf16[512,128]{1,0:T(8,128)(2,1)S(1)} %copy-done.18, bf16[8192,512]{1,0:T(8,128)(2,1)} %latent_ref.4, bf16[4096,128]{1,0:T(8,128)(2,1)S(1)} %gather_fusion.3, f32[128]{0:T(128)S(1)} %copy-done.19), kind=kOutput, calls=%fused_computation.18 | convolution fusion | flops 541589504 | bytes 8520192 | tf_op jit(solution)/shard_map/dot_general | solution.py:388
  209.2 0.0 all-gather.8.cloned.1.call-update
  209.9 0.7 pad_add_fusion.scalars.column
  210.6 0.6 fusion.28
  211.2 9.7 %all-gather.6.cloned.1.call-done.hidden_ref = bf16[4096,512]{1,0:T(8,128)(2,1)} async-done(((bf16[4096,128]{1,0:T(8,128)(2,1)}), bf16[4096,512]{1,0:T(8,128)(2,1)}) %all-gather.6.cloned.1.call-update) | async-done | bytes 4194320 | tf_op jit(solution)/shard_map/all_gather | solution.py:394
  220.8 8.0 %edge_finish.2 = (f32[4096,128]{1,0:T(8,128)}, bf16[4096,128]{1,0:T(8,128)(2,1)}) custom-call(s32[2]{0:T(128)} %pad_add_fusion.scalars.column, bf16[4096,512]{1,0:T(8,128)(2,1)} %all-gather.6.cloned.1.call-done.hidden_ref, bf16[8192,512]{1,0:T(8,128)(2,1)} %latent_ref.4, bf16[512,512]{1,0:T(8,128)(2,1)} %get-tuple-element.13.w_ref, ...), custom_call_target="tpu_custom_call" | custom-call | flops 2147483648 | bytes 8388608 | tf_op jit(solution)/shard_map/edge_finish/pallas_call | solution.py:53
  228.8 31.1 %scatter_custom_fusion = f32[40960,128]{1,0:T(8,128)} fusion(s32[4096]{0:T(1024)S(1)} %get-tuple-element.39, f32[4096,128]{1,0:T(8,128)} %get-tuple-element.15, f32[]{:T(128)} %constant.13.clone.1), kind=kCustom, calls=%fused_computation.6 | custom fusion | flops 524288 | bytes 20972032 | tf_op jit(solution)/shard_map/scatter-add | solution.py:406
  259.9 8.0 %edge_finish.3 = (f32[4096,128]{1,0:T(8,128)}, bf16[4096,128]{1,0:T(8,128)(2,1)}) custom-call(s32[2]{0:T(128)} %pad_add_fusion.scalars.column, bf16[4096,512]{1,0:T(8,128)(2,1)} %all-gather.8.cloned.1.call-done.hidden_ref, bf16[8192,512]{1,0:T(8,128)(2,1)} %latent_ref.4, bf16[512,512]{1,0:T(8,128)(2,1)} %get-tuple-element.13.w_ref, ...), custom_call_target="tpu_custom_call" | custom-call | flops 2147483648 | bytes 8388608 | tf_op jit(solution)/shard_map/edge_finish/pallas_call | solution.py:53
  267.9 34.4 %scatter_fusion = f32[40960,128]{1,0:T(8,128)} fusion(f32[40960,128]{1,0:T(8,128)} %scatter_custom_fusion, s32[4096]{0:T(1024)S(1)} %get-tuple-element.38, f32[4096,128]{1,0:T(8,128)} %get-tuple-element.16), kind=kCustom, calls=%fused_computation.5 | custom fusion | flops 524288 | bytes 6307840 | tf_op jit(solution)/shard_map/scatter-add | solution.py:406
  302.2 131.8 %combine.1.summed_ref = bf16[4,5120,128]{2,1,0:T(8,128)(2,1)S(1)} custom-call(f32[4,2,5120,128]{3,2,1,0:T(8,128)} %bitcast.15), custom_call_target="tpu_custom_call" | custom-call | tf_op jit(solution)/shard_map/combine/pallas_call | solution.py:278
  434.1 2.3 copy-done.2
  436.4 1.5 pad_maximum_fusion
  437.8 14.6 %mesh_finish.1 = bf16[5120,128]{1,0:T(8,128)(2,1)} custom-call(s32[2]{0:T(128)} %pad_add_fusion.scalars.column, bf16[5120,512]{1,0:T(8,128)(2,1)} %own_ref.1, bf16[5120,512]{1,0:T(8,128)(2,1)} %own_ref.1, bf16[4,5120,128]{2,1,0:T(8,128)(2,1)} %copy-done.2, bf16[512,512]{1,0:T(8,128)(2,1)} %get-tuple-element.17.w_in_ref, ...), custom_call_target="tpu_custom_call" | custom-call | flops 8053063680 | bytes 13107200 | tf_op jit(solution)/shard_map/mesh_finish/pallas_call | solution.py:98
  452.4 0.0 copy-done.1
  (42 shorter events, 0.3 us)
Async XLA Ops:
  7.2 16.2 %copy-start = (bf16[3072,512]{1,0:T(8,128)(2,1)S(1)}, bf16[3072,512]{1,0:T(8,128)(2,1)}, u32[]{:S(2)}) copy-start(bf16[3072,512]{1,0:T(8,128)(2,1)} %param.22) | copy-start | bytes 9437188
  7.2 5.4 %copy-start.15 = (f32[128]{0:T(128)S(1)}, f32[128]{0:T(128)}, u32[]{:S(2)}) copy-start(f32[128]{0:T(128)} %param.41) | copy-start | bytes 1540
  7.2 5.4 %copy-start.16 = (f32[128]{0:T(128)S(1)}, f32[128]{0:T(128)}, u32[]{:S(2)}) copy-start(f32[128]{0:T(128)} %param.39) | copy-start | bytes 1540
  7.2 5.4 %copy-start.17 = (f32[128]{0:T(128)S(1)}, f32[128]{0:T(128)}, u32[]{:S(2)}) copy-start(f32[128]{0:T(128)} %param.34) | copy-start | bytes 1540
  7.2 9.9 %copy-start.8 = (bf16[512,128]{1,0:T(8,128)(2,1)S(1)}, bf16[512,128]{1,0:T(8,128)(2,1)}, u32[]{:S(2)}) copy-start(bf16[512,128]{1,0:T(8,128)(2,1)} %param.37) | copy-start | bytes 393220
  7.2 12.1 %copy-start.7 = (bf16[128,512]{1,0:T(8,128)(2,1)S(1)}, bf16[128,512]{1,0:T(8,128)(2,1)}, u32[]{:S(2)}) copy-start(bf16[128,512]{1,0:T(8,128)(2,1)} %param.33) | copy-start | bytes 393220
  7.2 158.7 %all-gather.4.cloned.1.call-start = ((), (), s32[]{:S(2)}) async-start(), calls=%async_computation | async-start | bytes 11796480 | tf_op jit(solution)/shard_map/all_gather | solution.py:362
  12.5 10.9 %copy-start.13 = (s32[8192]{0:T(1024)S(1)}, s32[8192]{0:T(1024)}, u32[]{:S(2)}) copy-start(s32[8192]{0:T(1024)} %param.26) | copy-start | bytes 98308
  12.5 208.3 %all-gather.6.cloned.1.call-start = ((), (), s32[]{:S(2)}) async-start(), calls=%async_computation.1 | async-start | bytes 5242880 | tf_op jit(solution)/shard_map/all_gather | solution.py:394
  12.6 87.2 %collective-permute-start.8 = (f32[3,128]{1,0:T(4,128)S(1)}, f32[3,128]{1,0:T(4,128)S(1)}, u32[]{:S(2)}, u32[]{:S(2)}) collective-permute-start(f32[3,128]{1,0:T(4,128)S(1)} %pad_maximum_fusion.4), channel_id=1, source_target_pairs={{3,0},{0,1},{1,2},{2,3},{7,4},{4,5},{5,6},{6,7},{11,8},{8,9},{9,10... | collective-permute-start | bytes 4616 | tf_op jit(solution)/shard_map/ppermute | solution.py:312
  13.2 87.0 %collective-permute-start.7 = (f32[3,128]{1,0:T(4,128)S(1)}, f32[3,128]{1,0:T(4,128)S(1)}, u32[]{:S(2)}, u32[]{:S(2)}) collective-permute-start(f32[3,128]{1,0:T(4,128)S(1)} %pad_maximum_fusion.4), channel_id=1, source_target_pairs={{2,0},{3,1},{0,2},{1,3},{6,4},{7,5},{4,6},{5,7},{10,8},{11,9},{8,1... | collective-permute-start | bytes 4616 | tf_op jit(solution)/shard_map/ppermute | solution.py:312
  15.7 84.4 %collective-permute-start.6 = (f32[3,128]{1,0:T(4,128)S(1)}, f32[3,128]{1,0:T(4,128)S(1)}, u32[]{:S(2)}, u32[]{:S(2)}) collective-permute-start(f32[3,128]{1,0:T(4,128)S(1)} %pad_maximum_fusion.4), channel_id=1, source_target_pairs={{1,0},{2,1},{3,2},{0,3},{5,4},{6,5},{7,6},{4,7},{9,8},{10,9},{11,1... | collective-permute-start | bytes 4616 | tf_op jit(solution)/shard_map/ppermute | solution.py:312
  19.3 100.0 %collective-permute-start.5 = (bf16[1024,128]{1,0:T(8,128)(2,1)}, bf16[1024,128]{1,0:T(8,128)(2,1)}, u32[]{:S(2)}, u32[]{:S(2)}) collective-permute-start(bf16[1024,128]{1,0:T(8,128)(2,1)} %constant_dynamic-update-slice_fusion.4), channel_id=1, source_target_pairs={{3,0},{0,1},{1,2},{2,3},{7,4},{4,5},{5,6},{6,7},{11,8},{8,9},{9,10... | collective-permute-start | bytes 786440 | tf_op jit(solution)/shard_map/ppermute | solution.py:312
  21.6 80.3 %collective-permute-start = (bf16[256,512]{1,0:T(8,128)(2,1)}, bf16[256,512]{1,0:T(8,128)(2,1)}, u32[]{:S(2)}, u32[]{:S(2)}) collective-permute-start(bf16[256,512]{1,0:T(8,128)(2,1)} %constant_dynamic-update-slice_fusion), channel_id=1, source_target_pairs={{1,0},{2,1},{3,2},{0,3},{5,4},{6,5},{7,6},{4,7},{9,8},{10,9},{11,1... | collective-permute-start | bytes 786440 | tf_op jit(solution)/shard_map/ppermute | solution.py:312
  23.4 3.1 copy-start.14
  23.4 3.1 copy-start.3
  26.5 45.6 %copy-start.4 = (f32[3072,128]{1,0:T(8,128)S(1)}, f32[3072,128]{1,0:T(8,128)}, u32[]{:S(2)}) copy-start(f32[3072,128]{1,0:T(8,128)} %fusion.29) | copy-start | bytes 4718596
  72.1 30.1 %copy-start.12 = (bf16[1024,512]{1,0:T(8,128)(2,1)S(1)}, bf16[1024,512]{1,0:T(8,128)(2,1)}, u32[]{:S(2)}) copy-start(bf16[1024,512]{1,0:T(8,128)(2,1)} %get-tuple-element.35) | copy-start | bytes 3145732
  99.8 20.6 %collective-permute-start.4 = (bf16[1024,128]{1,0:T(8,128)(2,1)}, bf16[1024,128]{1,0:T(8,128)(2,1)S(1)}, u32[]{:S(2)}, u32[]{:S(2)}) collective-permute-start(bf16[1024,128]{1,0:T(8,128)(2,1)} %constant_dynamic-update-slice_fusion.4), channel_id=1, source_target_pairs={{2,0},{3,1},{0,2},{1,3},{6,4},{7,5},{4,6},{5,7},{10,8},{11,9},{8,1... | collective-permute-start | bytes 786440 | tf_op jit(solution)/shard_map/ppermute | solution.py:312
  100.1 20.4 %collective-permute-start.3 = (bf16[1024,128]{1,0:T(8,128)(2,1)}, bf16[1024,128]{1,0:T(8,128)(2,1)S(1)}, u32[]{:S(2)}, u32[]{:S(2)}) collective-permute-start(bf16[1024,128]{1,0:T(8,128)(2,1)} %constant_dynamic-update-slice_fusion.4), channel_id=1, source_target_pairs={{1,0},{2,1},{3,2},{0,3},{5,4},{6,5},{7,6},{4,7},{9,8},{10,9},{11,1... | collective-permute-start | bytes 786440 | tf_op jit(solution)/shard_map/ppermute | solution.py:312
  100.1 18.1 %collective-permute-start.1 = (bf16[256,512]{1,0:T(8,128)(2,1)}, bf16[256,512]{1,0:T(8,128)(2,1)S(1)}, u32[]{:S(2)}, u32[]{:S(2)}) collective-permute-start(bf16[256,512]{1,0:T(8,128)(2,1)} %constant_dynamic-update-slice_fusion), channel_id=1, source_target_pairs={{2,0},{3,1},{0,2},{1,3},{6,4},{7,5},{4,6},{5,7},{10,8},{11,9},{8,1... | collective-permute-start | bytes 786440 | tf_op jit(solution)/shard_map/ppermute | solution.py:312
  102.0 16.3 %collective-permute-start.2 = (bf16[256,512]{1,0:T(8,128)(2,1)}, bf16[256,512]{1,0:T(8,128)(2,1)S(1)}, u32[]{:S(2)}, u32[]{:S(2)}) collective-permute-start(bf16[256,512]{1,0:T(8,128)(2,1)} %constant_dynamic-update-slice_fusion), channel_id=1, source_target_pairs={{3,0},{0,1},{1,2},{2,3},{7,4},{4,5},{5,6},{6,7},{11,8},{8,9},{9,10... | collective-permute-start | bytes 786440 | tf_op jit(solution)/shard_map/ppermute | solution.py:312
  118.3 2.2 copy-start.9
  118.3 2.2 copy-start.10
  120.4 1.3 copy-start.11
  165.9 16.4 %copy-start.18 = (bf16[512,128]{1,0:T(8,128)(2,1)S(1)}, bf16[512,128]{1,0:T(8,128)(2,1)}, u32[]{:S(2)}) copy-start(bf16[512,128]{1,0:T(8,128)(2,1)} %param.29) | copy-start | bytes 393220
  165.9 16.4 %copy-start.19 = (f32[128]{0:T(128)S(1)}, f32[128]{0:T(128)}, u32[]{:S(2)}) copy-start(f32[128]{0:T(128)} %param.32) | copy-start | bytes 1540
  187.5 72.4 %all-gather.8.cloned.1.call-start = ((), (), s32[]{:S(2)}) async-start(), calls=%async_computation.2 | async-start | bytes 5242880 | tf_op jit(solution)/shard_map/all_gather | solution.py:394
  302.2 134.2 %copy-start.5 = (bf16[4096,128]{1,0:T(8,128)(2,1)S(1)}, bf16[4096,128]{1,0:T(8,128)(2,1)}, u32[]{:S(2)}) copy-start(bf16[4096,128]{1,0:T(8,128)(2,1)} %get-tuple-element.20) | copy-start | bytes 3145732
  302.2 134.2 %copy-start.6 = (bf16[4096,128]{1,0:T(8,128)(2,1)S(1)}, bf16[4096,128]{1,0:T(8,128)(2,1)}, u32[]{:S(2)}) copy-start(bf16[4096,128]{1,0:T(8,128)(2,1)} %get-tuple-element.21) | copy-start | bytes 3145732
  434.1 2.3 copy-start.2
  437.8 14.6 %copy-start.1 = (bf16[3072,512]{1,0:T(8,128)(2,1)S(1)}, bf16[3072,512]{1,0:T(8,128)(2,1)}, u32[]{:S(2)}) copy-start(bf16[3072,512]{1,0:T(8,128)(2,1)} %param.22) | copy-start | bytes 9437188
Sparse Core Ops, SparseCore 0:
  12.6 153.2 all-gather.3
  187.6 33.1 all-gather.5
  222.4 34.9 all-gather.7
